TPU v7x, 256 devices: a whole 4x4x8 slice. The times are simulated.
256 devices in a mesh: dp: 8 (over y, z_hi), fsdp: 32 (over x, z_lo, core).
Axes of the slice: x: 4, y: 4, z: 8 (z_hi: 2, z_lo: 4; z = z_hi * 4 + z_lo), core: 2. Of those that a mesh axis runs over, the one named last changes fastest.
Arguments:
- tokens: bfloat16 [98304, 1024], P(('dp', 'fsdp')), may hold values from -6.5 to 6.5
- cotangent: bfloat16 [98304, 1024], P(('dp', 'fsdp')), may hold values from -6 to 6
- patch_count: int32 [256], P(('dp', 'fsdp')), may hold values from 96 to 384, as said below
- image_starts: int32 [256, 8], P(('dp', 'fsdp')), may hold values from 0 to 384, as said below
- qkv_weight: bfloat16 [1024, 3072], P('fsdp'), may hold values from -8 to 8
- proj_weight: bfloat16 [1024, 1024], P('fsdp'), may hold values from -0.1875 to 0.1875
- norm_gain: bfloat16 [1024], P('fsdp'), may hold values from 0.25 to 1.75
- norm_shift: bfloat16 [1024], P('fsdp'), may hold values from -3 to 3
Outputs:
- grad_tokens: bfloat16 [98304, 1024], P(('dp', 'fsdp'))
- qkv_grad: float32 [1024, 3072], P('fsdp')
- proj_grad: float32 [1024, 1024], P('fsdp')
- gain_grad: float32 [1024], P('fsdp')
- shift_grad: float32 [1024], P('fsdp')
Inputs may be any that keep to these rules, and one draw needn't show every extreme that they name: `patch_count`: at least one device has all 384 slots live; live slots of a device come first. `image_starts`: per device, non-decreasing and first 0; an image runs from its start to the next start or to the device's patch count; a start equal to the patch count marks an absent image; no image has more than 192 patches.
All inputs are finite; a program needn't handle non-finite values.
Results may differ from a plain program's by a relative error of at most 0.025.
The roundings to bfloat16 on the way count: a program that leaves them out, or rounds other values in their place, can miss the bound.
Values may be sent and summed in bfloat16 or wider, within the bound.
A program may use at most 128 MiB of HBM per device.

v0:
```python
import math

import jax
import jax.numpy as jnp
from jax import lax
from jax.sharding import PartitionSpec as P

D = 1024
HEAD_DIM = 64
HEADS = 16


norm_eps = 1e-06
masked_score = -1e30


def side_by_side(arrays, axis, dim, along):
    columns = [a.reshape(*a.shape[:along], -1) for a in arrays]
    both = jnp.concatenate(columns, axis=along)
    result, at, done = (lax.all_gather(both, axis, axis=dim, tiled=True), 0, [])
    for a, column in zip(arrays, columns):
        share = result[..., at : at + column.shape[along]]
        done.append(share.reshape(*share.shape[:along], *a.shape[along:]))
        at += column.shape[along]
    return tuple(done)


def sent_together(arrays, axis, dim, along):
    widths = [math.prod(a.shape[along:]) for a in arrays]
    both = jnp.concatenate(
        [a.reshape(*a.shape[:along], w) for a, w in zip(arrays, widths)], axis=along
    )
    result = lax.psum_scatter(both, axis, scatter_dimension=dim, tiled=True)
    parts = jnp.split(result, [sum(widths[:k]) for k in range(1, len(widths))], axis=along)
    return tuple(
        (b.reshape(*result.shape[:along], *a.shape[along:]) for a, b in zip(arrays, parts))
    )


def copy_for_each(shard, axis):
    size = lax.axis_size(axis)
    return lax.all_to_all(
        jnp.broadcast_to(shard[None], (size, *shard.shape)), axis, 0, 0, tiled=True
    )


def over_copies(shard, axis):
    everything = copy_for_each(shard, axis)
    return jnp.sum(everything.astype(jnp.float32), axis=0)


def block_backward(
    block_tokens, block_cot, live_count, starts, qkv_weight, proj_weight, norm_gain, norm_shift
):
    rows = block_tokens.shape[0]
    factor = HEAD_DIM ** (-0.5)
    position = jnp.arange(rows, dtype=jnp.int32)
    live = position < live_count
    segment = jnp.sum((starts[None, :] <= position[:, None]).astype(jnp.int32), axis=1)
    allowed = live[:, None] & live[None, :] & (segment[:, None] == segment[None, :])
    source = block_tokens.astype(jnp.float32)
    center = jnp.mean(source, axis=1, keepdims=True)
    centered = source - center
    variance = jnp.mean(centered * centered, axis=1, keepdims=True)
    inverse = lax.rsqrt(variance + norm_eps)
    normed = centered * inverse
    gain = norm_gain.astype(jnp.float32)
    hidden = (normed * gain + norm_shift.astype(jnp.float32)).astype(jnp.bfloat16)
    qkv = jnp.dot(hidden, qkv_weight, preferred_element_type=jnp.float32).astype(jnp.bfloat16)
    split = qkv.reshape(rows, 3, HEADS, HEAD_DIM)
    queries = split[:, 0]
    keys = split[:, 1]
    values = split[:, 2]
    scores = jnp.einsum("qhe,khe->hqk", queries, keys, preferred_element_type=jnp.float32) * factor
    scores = jnp.where(allowed[None], scores, masked_score)
    row_max = jnp.max(scores, axis=2, keepdims=True)
    expon = jnp.exp(scores - row_max)
    probs = expon / jnp.sum(expon, axis=2, keepdims=True)
    probs_low = probs.astype(jnp.bfloat16)
    attended = (
        jnp.einsum("hqk,khe->qhe", probs_low, values, preferred_element_type=jnp.float32)
        .reshape(rows, D)
        .astype(jnp.bfloat16)
    )
    masked_cot = jnp.where(live[:, None], block_cot, jnp.zeros_like(block_cot))
    proj_term = jnp.dot(attended.T, masked_cot, preferred_element_type=jnp.float32)
    grad_attended = jnp.dot(masked_cot, proj_weight.T, preferred_element_type=jnp.float32).astype(
        jnp.bfloat16
    )
    grad_heads = grad_attended.reshape(rows, HEADS, HEAD_DIM)
    grad_probs = jnp.einsum("qhe,khe->hqk", grad_heads, values, preferred_element_type=jnp.float32)
    grad_values = jnp.einsum(
        "hqk,qhe->khe", probs_low, grad_heads, preferred_element_type=jnp.float32
    ).astype(jnp.bfloat16)
    grad_scores = probs * (grad_probs - jnp.sum(probs * grad_probs, axis=2, keepdims=True)) * factor
    grad_scores = grad_scores.astype(jnp.bfloat16)
    grad_queries = jnp.einsum(
        "hqk,khe->qhe", grad_scores, keys, preferred_element_type=jnp.float32
    ).astype(jnp.bfloat16)
    grad_keys = jnp.einsum(
        "hqk,qhe->khe", grad_scores, queries, preferred_element_type=jnp.float32
    ).astype(jnp.bfloat16)
    grad_qkv = jnp.stack([grad_queries, grad_keys, grad_values], axis=1).reshape(rows, 3 * D)
    qkv_term = jnp.dot(hidden.T, grad_qkv, preferred_element_type=jnp.float32)
    grad_hidden = jnp.dot(grad_qkv, qkv_weight.T, preferred_element_type=jnp.float32)
    gain_term = jnp.sum(grad_hidden * normed, axis=0)
    shift_term = jnp.sum(grad_hidden, axis=0)
    grad_normed = grad_hidden * gain
    inner = grad_normed - jnp.mean(grad_normed, axis=1, keepdims=True)
    inner = inner - normed * jnp.mean(grad_normed * normed, axis=1, keepdims=True)
    grad_block = (block_cot.astype(jnp.float32) + inverse * inner).astype(jnp.bfloat16)
    return (grad_block, qkv_term, proj_term, gain_term, shift_term)


def per_device(
    tokens, cotangent, patch_count, image_starts, qkv_weight, proj_weight, norm_gain, norm_shift
):
    whole_qkv, whole_proj, whole_gain, whole_shift = side_by_side(
        (qkv_weight, proj_weight, norm_gain, norm_shift), "fsdp", 0, 1
    )
    grad_block, qkv_term, proj_term, gain_term, shift_term = block_backward(
        tokens,
        cotangent,
        patch_count[0],
        image_starts[0],
        whole_qkv,
        whole_proj,
        whole_gain,
        whole_shift,
    )
    replicas = lax.axis_size("dp")
    owners = lax.axis_size("fsdp")
    factor = 1.0 / math.sqrt(tokens.shape[0] * replicas * owners)
    terms = (qkv_term, proj_term, gain_term, shift_term)
    summed = tuple(
        (
            part.astype(jnp.float32)
            for part in sent_together(
                (
                    terms[0].astype(jnp.bfloat16),
                    terms[1].astype(jnp.bfloat16),
                    terms[2].astype(jnp.bfloat16),
                    terms[3].astype(jnp.bfloat16),
                ),
                "fsdp",
                0,
                1,
            )
        )
    )
    summed = (
        over_copies(summed[0].astype(jnp.bfloat16), "dp").astype(jnp.float32),
        over_copies(summed[1].astype(jnp.bfloat16), "dp").astype(jnp.float32),
        over_copies(summed[2].astype(jnp.bfloat16), "dp").astype(jnp.float32),
        over_copies(summed[3].astype(jnp.bfloat16), "dp").astype(jnp.float32),
    )
    return (
        grad_block,
        summed[0] * factor,
        summed[1] * factor,
        summed[2] * factor,
        summed[3] * factor,
    )


def solution(mesh):
    placed = (
        P(("dp", "fsdp"), None),
        P(("dp", "fsdp"), None),
        P(("dp", "fsdp")),
        P(("dp", "fsdp"), None),
        P("fsdp", None),
        P("fsdp", None),
        P("fsdp"),
        P("fsdp"),
    )
    return jax.shard_map(
        per_device,
        mesh=mesh,
        in_specs=placed,
        out_specs=(P(("dp", "fsdp"), None), P("fsdp", None), P("fsdp", None), P("fsdp"), P("fsdp")),
        check_vma=False,
    )
```

profile of v0, /device:TPU:32, one launch (start us, length us, event | category | flops | bytes accessed | tf_op | source)
XLA Modules:
  0.0 420.0 jit_solution(583153448103038332)
XLA Ops:
  7.2 0.0 copy-start.5
  7.2 0.0 all-gather.2.cloned.1.call-start
  7.2 0.8 copy.60
  8.0 0.8 copy.61
  8.8 1.7 concatenate.6
  10.5 0.0 all-gather.2.cloned.1.call-update
  10.5 0.0 reduce-scatter.2.cloned.1.call-start
  11.2 0.7 convert_reduce_fusion.5
  12.0 1.3 convert_reduce_fusion.1
  13.3 1.5 fusion.42
  14.8 0.2 compare_and_fusion
  15.0 0.0 copy-start
  15.0 66.5 %all-gather.2.cloned.1.call-done = bf16[1024,4098]{1,0:T(8,128)(2,1)} async-done(((bf16[32,4098]{1,0:T(8,128)(2,1)}), bf16[1024,4098]{1,0:T(8,128)(2,1)}) %all-gather.2.cloned.1.call-update) | async-done | bytes 8392720 | tf_op jit(solution)/shard_map/all_gather | solution.py:20
  81.5 0.0 copy-done.5
  81.5 2.6 fusion.55
  84.1 1.2 copy.63
  85.3 1.4 convert_reduce_fusion.4
  86.6 0.0 copy-done
  86.6 6.9 %fusion.19 = bf16[384,3072]{1,0:T(8,128)(2,1)} fusion(bf16[1024,4098]{1,0:T(8,128)(2,1)} %all-gather.2.cloned.1.call-done, bf16[384,1024]{1,0:T(8,128)(2,1)S(1)} %copy-done, f32[1024]{0:T(1024)S(1)} %get-tuple-element.6, f32[1024]{0:T(1024)S(1)} %get-tuple-element.5, f32[384]{0:T(512)S(1)} %add_rsqrt_fusion, f32[384]{0:T(512)S(1)} %broadcast_multiply_fusion.4), kind=kOutput, calls=%fused_computation.19 | convolution fusion | flops 2419458048 | bytes 9448448 | tf_op jit(solution)/shard_map/dot_general | solution.py:69
  93.6 3.0 copy.62
  96.6 5.6 %fusion.81 = (f32[16,384]{1,0:T(8,128)S(1)}, f32[16,384,384]{1,2,0:T(8,128)}) fusion(pred[384,384]{0,1:T(8,128)(4,1)S(1)} %compare_and_fusion, bf16[384,3,16,64]{0,3,2,1:T(8,128)(2,1)S(1)} %bitcast.56), kind=kOutput, calls=%fused_computation.89 | convolution fusion | flops 311427456 | bytes 11182080 | tf_op jit(solution)/shard_map/sub | solution.py:77
  102.2 6.4 %fusion.69 = f32[16,384,384]{1,2,0:T(8,128)} fusion(bf16[384,16,64]{0,2,1:T(8,128)(2,1)} %bitcast.61, bf16[384,3,16,64]{0,3,2,1:T(8,128)(2,1)S(1)} %bitcast.57), kind=kOutput, calls=%fused_computation.61 | convolution fusion | flops 301989888 | bytes 11010048 | tf_op jit(solution)/shard_map/qhe,khe->hqk/dot_general | solution.py:91
  108.5 0.0 copy-done.1
  108.5 0.0 copy-done.7
  108.5 2.7 fusion.64
  111.2 14.4 %fusion.58 = bf16[384,1,16,64]{0,3,2,1:T(8,128)(2,1)} fusion(f32[16,384,384]{1,2,0:T(8,128)} %fusion.69, bf16[384,3,16,64]{0,3,2,1:T(8,128)(2,1)S(1)} %bitcast.58, f32[16,384,384]{1,2,0:T(8,128)} %get-tuple-element.14, f32[16,384]{1,0:T(8,128)S(1)} %get-tuple-element.13), kind=kOutput, calls=%fused_computation.52 | convolution fusion | flops 318904704 | bytes 39370752 | tf_op jit(solution)/shard_map/hqk,qhe->khe/dot_general | solution.py:100
  125.7 15.6 %fusion.61 = bf16[384,1,16,64]{0,3,2,1:T(8,128)(2,1)} fusion(f32[16,384,384]{1,2,0:T(8,128)} %fusion.69, bf16[384,3,16,64]{0,3,2,1:T(8,128)(2,1)S(1)} %bitcast.59, f32[16,384,384]{1,2,0:T(8,128)} %get-tuple-element.14, f32[16,384]{1,0:T(8,128)S(1)} %get-tuple-element.13), kind=kOutput, calls=%fused_computation.53 | convolution fusion | flops 318904704 | bytes 39370752 | tf_op jit(solution)/shard_map/hqk,khe->qhe/dot_general | solution.py:97
  141.2 4.7 %fusion.46 = bf16[16,64,384]{2,1,0:T(8,128)(2,1)S(1)} fusion(bf16[384,3,16,64]{0,3,2,1:T(8,128)(2,1)S(1)} %bitcast.60, f32[16,384,384]{1,2,0:T(8,128)} %get-tuple-element.14, f32[16,384]{1,0:T(8,128)S(1)} %get-tuple-element.13), kind=kOutput, calls=%fused_computation.47 | convolution fusion | flops 307101696 | bytes 11034624 | tf_op jit(solution)/shard_map/hqk,khe->qhe/dot_general | solution.py:81
  145.9 0.0 copy-done.2
  146.0 0.0 copy-done.3
  146.0 0.0 slice-start
  146.0 0.3 pad_maximum_fusion
  146.3 0.0 copy-start.6
  146.3 0.0 slice-start.1
  146.3 0.0 slice-start.2
  146.3 6.0 %convolution_convert_fusion = bf16[1024,3072]{1,0:T(8,128)(2,1)} fusion(bf16[384,3072]{0,1:T(8,128)(2,1)S(1)} %bitcast.63, bf16[384,1024]{1,0:T(8,128)(2,1)S(1)} %copy-done, f32[1024]{0:T(1024)S(1)} %get-tuple-element.6, f32[1024]{0:T(1024)S(1)} %get-tuple-element.5, f32[384]{0:T(512)S(1)} %add_rsqrt_fusion, f32[384]{0:T(512)S(1)} %broadcast_multiply_fusion.4), kind=kOutput, calls=%fused_computation.8 | convolution fusion | flops 2421424128 | bytes 9448448 | tf_op jit(solution)/shard_map/dot_general | solution.py:104
  152.3 0.0 copy-done.6
  152.3 1.3 convolution_convert_fusion.1
  153.7 4.1 fusion.41
  157.8 0.2 convert_element_type.162
  158.0 0.2 convert_element_type.163
  158.2 13.0 %concatenate.7 = bf16[1024,4098]{1,0:T(8,128)(2,1)} concatenate(bf16[1024,3072]{1,0:T(8,128)(2,1)} %convolution_convert_fusion, bf16[1024,1024]{1,0:T(8,128)(2,1)S(1)} %convolution_convert_fusion.1, bf16[1024,1]{1,0:T(8,128)(2,1)S(1)} %convert_element_type.162, bf16[1024,1]{1,0:T(8,128)(2,1)S(1)} %convert_element_type.163), dimensions={1} | concatenate | bytes 16785408 | tf_op jit(solution)/shard_map/concatenate | solution.py:30
  171.3 0.0 reduce-scatter.2.cloned.1.call-update
  171.3 158.2 %reduce-scatter.2.cloned.1.call-done = bf16[32,4098]{1,0:T(8,128)(2,1)} async-done(((bf16[1024,4098]{1,0:T(8,128)(2,1)}), bf16[32,4098]{1,0:T(8,128)(2,1)}) %reduce-scatter.2.cloned.1.call-update) | async-done | bytes 262288 | tf_op jit(solution)/shard_map/reduce_scatter | solution.py:33
  329.5 1.0 slice_reduce_fusion
  330.4 17.1 %all_to_all.22 = bf16[8,1,32]{2,1,0:T(2,128)(2,1)S(1)} all-to-all(bf16[8,1,32]{2,1,0:T(2,128)(2,1)S(1)} %broadcast_in_dim.41), channel_id=1, replica_groups=mesh['dp'=8,'fsdp'=32] {'dp'}, dimensions={0} | all-to-all | bytes 1024 | tf_op jit(solution)/shard_map/all_to_all | solution.py:42
  347.6 0.6 broadcast_in_dim.43
  348.2 3.3 all-to-all-start.3
  351.5 0.8 split.17
  352.3 9.2 %all-to-all-done.3 = bf16[8,1,32]{2,1,0:T(2,128)(2,1)S(1)} async-done(((bf16[8,1,32]{2,1,0:T(2,128)(2,1)}), bf16[8,1,32]{2,1,0:T(2,128)(2,1)S(1)}, u32[]{:S(2)}, u32[]{:S(2)}) %all-to-all-start.3) | async-done | bytes 544 | tf_op jit(solution)/shard_map/all_to_all | solution.py:42
  361.5 0.9 broadcast_in_dim.39
  362.4 3.5 all-to-all-start.1
  365.9 0.9 split.16
  366.8 15.4 %all-to-all-done.1 = bf16[8,32,1024]{2,1,0:T(8,128)(2,1)S(1)} async-done(((bf16[8,32,1024]{2,1,0:T(8,128)(2,1)}), bf16[8,32,1024]{2,1,0:T(8,128)(2,1)S(1)}, u32[]{:S(2)}, u32[]{:S(2)}) %all-to-all-start.1) | async-done | bytes 524320 | tf_op jit(solution)/shard_map/all_to_all | solution.py:42
  382.2 1.3 broadcast_in_dim.38
  383.5 4.9 %all-to-all-start = ((bf16[8,32,3072]{2,1,0:T(8,128)(2,1)}), bf16[8,32,3072]{2,1,0:T(8,128)(2,1)S(1)}, u32[]{:S(2)}, u32[]{:S(2)}) async-start(bf16[8,32,3072]{2,1,0:T(8,128)(2,1)} %broadcast_in_dim.38), calls=%async_computation.1 | async-start | bytes 3145728 | tf_op jit(solution)/shard_map/all_to_all | solution.py:42
  388.4 3.2 fusion.40
  391.7 0.5 broadcast_multiply_fusion.6
  392.2 0.5 broadcast_multiply_fusion.5
  392.7 0.1 convert_reduce_fusion.2
  392.8 0.7 broadcast_multiply_fusion.1
  393.4 18.7 %all-to-all-done = bf16[8,32,3072]{2,1,0:T(8,128)(2,1)S(1)} async-done(((bf16[8,32,3072]{2,1,0:T(8,128)(2,1)}), bf16[8,32,3072]{2,1,0:T(8,128)(2,1)S(1)}, u32[]{:S(2)}, u32[]{:S(2)}) %all-to-all-start) | async-done | bytes 1572896 | tf_op jit(solution)/shard_map/all_to_all | solution.py:42
  412.1 0.2 convert_reduce_fusion
  412.3 0.8 broadcast_multiply_fusion
  (17 shorter events, 0.1 us)
Async XLA Ops:
  7.2 74.3 %copy-start.5 = (bf16[384,1024]{1,0:T(8,128)(2,1)S(1)}, bf16[384,1024]{1,0:T(8,128)(2,1)}, u32[]{:S(2)}) copy-start(bf16[384,1024]{1,0:T(8,128)(2,1)} %param.9) | copy-start | bytes 2359300
  7.2 74.3 %all-gather.2.cloned.1.call-start = ((), (), s32[]{:S(2)}) async-start(), calls=%async_computation.5 | async-start | bytes 8921088 | tf_op jit(solution)/shard_map/all_gather | solution.py:20
  10.5 318.9 %reduce-scatter.2.cloned.1.call-start = ((), (), s32[]{:S(2)}) async-start(), calls=%async_computation.6 | async-start | bytes 8921088 | tf_op jit(solution)/shard_map/reduce_scatter | solution.py:33
  15.0 71.6 %copy-start = (bf16[384,1024]{1,0:T(8,128)(2,1)S(1)}, bf16[384,1024]{1,0:T(8,128)(2,1)}, u32[]{:S(2)}) copy-start(bf16[384,1024]{1,0:T(8,128)(2,1)} %param.8) | copy-start | bytes 2359300
  102.2 6.4 %copy-start.1 = (bf16[384,1024]{0,1:T(8,128)(2,1)S(1)}, bf16[384,1024]{0,1:T(8,128)(2,1)}, u32[]{:S(2)}) copy-start(bf16[384,1024]{0,1:T(8,128)(2,1)} %copy.63) | copy-start | bytes 2359300
  102.2 6.4 %copy-start.7 = (f32[16,384,384]{1,2,0:T(8,128)S(1)}, f32[16,384,384]{1,2,0:T(8,128)}, u32[]{:S(2)}) copy-start(f32[16,384,384]{1,2,0:T(8,128)} %get-tuple-element.14) | copy-start | bytes 28311556
  141.2 4.7 %copy-start.2 = (bf16[384,1,16,64]{0,3,2,1:T(8,128)(2,1)S(1)}, bf16[384,1,16,64]{0,3,2,1:T(8,128)(2,1)}, u32[]{:S(2)}) copy-start(bf16[384,1,16,64]{0,3,2,1:T(8,128)(2,1)} %fusion.64) | copy-start | bytes 2359300
  141.2 4.7 %copy-start.3 = (bf16[384,1,16,64]{0,3,2,1:T(8,128)(2,1)S(1)}, bf16[384,1,16,64]{0,3,2,1:T(8,128)(2,1)}, u32[]{:S(2)}) copy-start(bf16[384,1,16,64]{0,3,2,1:T(8,128)(2,1)} %fusion.58) | copy-start | bytes 2359300
  141.2 4.7 %copy-start.4 = (bf16[384,1,16,64]{0,3,2,1:T(8,128)(2,1)S(1)}, bf16[384,1,16,64]{0,3,2,1:T(8,128)(2,1)}, u32[]{:S(2)}) copy-start(bf16[384,1,16,64]{0,3,2,1:T(8,128)(2,1)} %fusion.61) | copy-start | bytes 2359300
  146.0 7.7 %slice-start = ((s8[8650752]{0:T(1024)(128)(4,1)}), s8[4194304]{0:T(1024)(128)(4,1)S(1)}, s32[]{:S(2)}) async-start(s8[8650752]{0:T(1024)(128)(4,1)} %bitcast.65), calls=%async_computation.7 | async-start | bytes 8388608
  146.3 6.0 %copy-start.6 = (bf16[384,1024]{1,0:T(8,128)(2,1)S(1)}, bf16[384,1024]{1,0:T(8,128)(2,1)}, u32[]{:S(2)}) copy-start(bf16[384,1024]{1,0:T(8,128)(2,1)} %param.9) | copy-start | bytes 2359300
  146.3 7.3 %slice-start.1 = ((s8[8650752]{0:T(1024)(128)(4,1)}), s8[4194304]{0:T(1024)(128)(4,1)S(1)}, s32[]{:S(2)}) async-start(s8[8650752]{0:T(1024)(128)(4,1)} %bitcast.65), calls=%async_computation.8 | async-start | bytes 8388608
  146.3 7.3 %slice-start.2 = ((s8[8650752]{0:T(1024)(128)(4,1)}), s8[262144]{0:T(1024)(128)(4,1)S(1)}, s32[]{:S(2)}) async-start(s8[8650752]{0:T(1024)(128)(4,1)} %bitcast.65), calls=%async_computation.9 | async-start | bytes 524288
  348.2 13.4 %all-to-all-start.3 = ((bf16[8,1,32]{2,1,0:T(2,128)(2,1)}), bf16[8,1,32]{2,1,0:T(2,128)(2,1)S(1)}, u32[]{:S(2)}, u32[]{:S(2)}) async-start(bf16[8,1,32]{2,1,0:T(2,128)(2,1)} %broadcast_in_dim.43), calls=%async_computation.4 | async-start | bytes 8192 | tf_op jit(solution)/shard_map/all_to_all | solution.py:42
  362.4 19.8 %all-to-all-start.1 = ((bf16[8,32,1024]{2,1,0:T(8,128)(2,1)}), bf16[8,32,1024]{2,1,0:T(8,128)(2,1)S(1)}, u32[]{:S(2)}, u32[]{:S(2)}) async-start(bf16[8,32,1024]{2,1,0:T(8,128)(2,1)} %broadcast_in_dim.39), calls=%async_computation.2 | async-start | bytes 1048576 | tf_op jit(solution)/shard_map/all_to_all | solution.py:42
  383.5 28.6 %all-to-all-start = ((bf16[8,32,3072]{2,1,0:T(8,128)(2,1)}), bf16[8,32,3072]{2,1,0:T(8,128)(2,1)S(1)}, u32[]{:S(2)}, u32[]{:S(2)}) async-start(bf16[8,32,3072]{2,1,0:T(8,128)(2,1)} %broadcast_in_dim.38), calls=%async_computation.1 | async-start | bytes 3145728 | tf_op jit(solution)/shard_map/all_to_all | solution.py:42
Sparse Core Ops, SparseCore 0:
  10.7 70.7 all-gather.1
  171.4 158.0 reduce-scatter.1
where the time goes:
time: 428 us; the launch traced here: 420 us
  waiting for transfers between devices  268 us (63%)
  matrix products  70.3 us (16%)
  local copies, waits for them, and re-layouts  26.5 us (6%)
  blocking collectives  17.1 us (4%)
  between operations  14.9 us (3%)
  starting transfers between devices  11.8 us (3%)
  other arithmetic  11.4 us (3%)
    reduce_scatter x1, waiting for transfers between devices, sent_together(): result = lax.psum_scatter(both, axis, scatter_dimension=dim, tiled=True)  158 us
    all_gather x1, waiting for transfers between devices, side_by_side(): result, at, done = (lax.all_gather(both, axis, axis=dim, tiled=True), 0, [])  66.5 us
    all_to_all x3, waiting for transfers between devices, copy_for_each(): lax.all_to_all(jnp.broadcast_to(shard[None], (size, *shard.shape)), axis,...  43.2 us
    all_to_all x1, blocking collectives, copy_for_each(): lax.all_to_all(jnp.broadcast_to(shard[None], (size, *shard.shape)), axis,...  17.1 us
    dot_general x1, matrix products, block_backward(): jnp.einsum('hqk,khe->qhe', grad_scores, keys, preferred_element_type=jnp....  15.6 us
    dot_general x1, matrix products, block_backward(): jnp.einsum('hqk,qhe->khe', grad_scores, queries, preferred_element_type=j...  14.4 us
    concatenate x1, local copies, waits for them, and re-layouts, sent_together(): jnp.concatenate([a.reshape(*a.shape[:along], w) for a, w in zip(arrays, w...  13 us
    all_to_all x3, starting transfers between devices, copy_for_each(): lax.all_to_all(jnp.broadcast_to(shard[None], (size, *shard.shape)), axis,...  11.7 us
  transfers between devices with their start and end apart: 5, of which 5 were waited for; matrix products, arithmetic and copies ran while one was open for 3% of the time, Pallas kernels for 0%

commit v1 on v0

--- a/solution.py
+++ b/solution.py
@@ -1,52 +1,441 @@
+import functools
 import math
 
 import jax
 import jax.numpy as jnp
 from jax import lax
+from jax.experimental import pallas as pl
+from jax.experimental.pallas import tpu as pltpu
 from jax.sharding import PartitionSpec as P
 
 D = 1024
 HEAD_DIM = 64
 HEADS = 16
-
+MESH = pl.DeviceIdType.MESH
+F32 = jnp.float32
+BF16 = jnp.bfloat16
 
 norm_eps = 1e-06
 masked_score = -1e30
 
 
-def side_by_side(arrays, axis, dim, along):
-    columns = [a.reshape(*a.shape[:along], -1) for a in arrays]
-    both = jnp.concatenate(columns, axis=along)
-    result, at, done = (lax.all_gather(both, axis, axis=dim, tiled=True), 0, [])
-    for a, column in zip(arrays, columns):
-        share = result[..., at : at + column.shape[along]]
-        done.append(share.reshape(*share.shape[:along], *a.shape[along:]))
-        at += column.shape[along]
-    return tuple(done)
-
-
-def sent_together(arrays, axis, dim, along):
-    widths = [math.prod(a.shape[along:]) for a in arrays]
-    both = jnp.concatenate(
-        [a.reshape(*a.shape[:along], w) for a, w in zip(arrays, widths)], axis=along
-    )
-    result = lax.psum_scatter(both, axis, scatter_dimension=dim, tiled=True)
-    parts = jnp.split(result, [sum(widths[:k]) for k in range(1, len(widths))], axis=along)
-    return tuple(
-        (b.reshape(*result.shape[:along], *a.shape[along:]) for a, b in zip(arrays, parts))
-    )
-
-
-def copy_for_each(shard, axis):
-    size = lax.axis_size(axis)
-    return lax.all_to_all(
-        jnp.broadcast_to(shard[None], (size, *shard.shape)), axis, 0, 0, tiled=True
-    )
-
-
-def over_copies(shard, axis):
-    everything = copy_for_each(shard, axis)
-    return jnp.sum(everything.astype(jnp.float32), axis=0)
+class Place:
+    def __init__(self):
+        dp, fsdp = lax.axis_index("dp"), lax.axis_index("fsdp")
+        self.dp, self.fsdp = dp, fsdp
+        self.y, self.zhi = dp // 2, dp % 2
+        self.c = fsdp % 2
+        chip = fsdp // 2
+        self.x, self.zlo = chip // 4, chip % 4
+        self.z = self.zhi * 4 + self.zlo
+
+    def at(self, dx=0, dy=0, dz=0, flip=0):
+        x = (self.x + dx + 4) % 4
+        y = (self.y + dy + 4) % 4
+        z = (self.z + dz + 8) % 8
+        c = self.c + flip * (1 - 2 * self.c)
+        return {"dp": y * 2 + z // 4, "fsdp": (x * 4 + z % 4) * 2 + c}
+
+    def along_x(self, d):
+        return self.at(dx=(1 - self.c) * d, dz=self.c * d)
+
+    def along_z(self, d):
+        return self.at(dx=self.c * d, dz=(1 - self.c) * d)
+
+    def chip(self, i, j):
+        x = (self.x + (1 - self.c) * i + self.c * j + 8) % 4
+        z = (self.zlo + self.c * i + (1 - self.c) * j + 8) % 4
+        return x * 4 + z
+
+    def sibling(self):
+        return self.at(flip=1)
+
+    def partner(self):
+        return self.at(dz=4)
+
+
+def enter(devices):
+    barrier = pltpu.get_barrier_semaphore()
+    for device in devices:
+        pl.semaphore_signal(barrier, inc=1, device_id=device, device_id_type=MESH)
+    pl.semaphore_wait(barrier, len(devices))
+
+
+def send(src, dst, send_sem, recv_sem, device):
+    return pltpu.make_async_remote_copy(
+        src_ref=src,
+        dst_ref=dst,
+        send_sem=send_sem,
+        recv_sem=recv_sem,
+        device_id=device,
+        device_id_type=MESH,
+    )
+
+
+GATHER_SEMS = 36
+
+
+class Gather:
+    def __init__(self, place, buffer, send_sems, recv_sems):
+        self.place, self.buffer = place, buffer
+        self.send_sems, self.recv_sems = send_sems, recv_sems
+        self.sent = []
+
+    def block(self, i, j, rows=None):
+        ref = self.buffer.at[self.place.chip(i, j), self.place.c]
+        return ref if rows is None else ref.at[pl.ds(rows * 16, 16)]
+
+    def copy(self, src, index, device):
+        return send(src, src, self.send_sems.at[index], self.recv_sems.at[index], device)
+
+    def start(self, src, index, device):
+        copy = self.copy(src, index, device)
+        copy.start()
+        self.sent.append(copy)
+
+    def arrived(self, ref, index):
+        self.copy(ref, index, self.place.sibling()).wait_recv()
+
+    def to_second(self, i):
+        at = self.place
+        self.start(self.block(i, 0), 4 + 4 * (i % 4), at.along_z(1))
+        self.start(self.block(i, 0), 5 + 4 * (i % 4), at.along_z(-1))
+        self.to_sibling(i, 0)
+
+    def to_sibling(self, i, j):
+        self.start(self.block(i, j), 20 + 4 * (i % 4) + (j % 4), self.place.sibling())
+
+    def stage0(self):
+        at = self.place
+        self.start(self.block(0, 0), 0, at.along_x(1))
+        self.start(self.block(0, 0), 1, at.along_x(-1))
+        self.to_second(0)
+
+    def stage1(self):
+        at = self.place
+        self.arrived(self.block(-1, 0), 0)
+        self.start(self.block(-1, 0, 0), 2, at.along_x(1))
+        self.arrived(self.block(1, 0), 1)
+        self.start(self.block(1, 0, 1), 3, at.along_x(-1))
+        self.to_second(-1)
+        self.to_second(1)
+
+    def stage2(self):
+        self.arrived(self.block(2, 0, 0), 2)
+        self.arrived(self.block(2, 0, 1), 3)
+        self.to_second(2)
+
+    def stage3(self, i):
+        at = self.place
+        k = i % 4
+        self.arrived(self.block(i, -1), 4 + 4 * k)
+        self.start(self.block(i, -1, 0), 6 + 4 * k, at.along_z(1))
+        self.to_sibling(i, -1)
+        self.arrived(self.block(i, 1), 5 + 4 * k)
+        self.start(self.block(i, 1, 1), 7 + 4 * k, at.along_z(-1))
+        self.to_sibling(i, 1)
+
+    def stage4(self, i):
+        k = i % 4
+        self.arrived(self.block(i, 2, 0), 6 + 4 * k)
+        self.arrived(self.block(i, 2, 1), 7 + 4 * k)
+        self.to_sibling(i, 2)
+
+    def stage5(self):
+        at = self.place
+        for i in range(4):
+            for j in range(4):
+                ref = self.buffer.at[at.chip(j, i), 1 - at.c]
+                self.arrived(ref, 20 + 4 * i + j)
+        for copy in self.sent:
+            copy.wait_send()
+
+    def neighbours(self):
+        at = self.place
+        return [at.along_x(1), at.along_x(-1), at.along_z(1), at.along_z(-1), at.sibling()]
+
+
+ORDER = (0, -1, 1, 2)
+
+
+def gather_kernel(qkv_ref, proj_ref, small_ref, qkv_out, proj_out, small_out, *scratch):
+    place = Place()
+    sems = scratch[-3:]
+    buffers = scratch[:-3]
+    own = (qkv_ref, proj_ref, small_ref)
+    outs = (qkv_out, proj_out, small_out)
+    me = place.chip(0, 0)
+    local = []
+    for k, (src, buffer) in enumerate(zip(own, buffers)):
+        copy = pltpu.make_async_copy(src, buffer.at[me, place.c], sems[2].at[k])
+        copy.start()
+        local.append(copy)
+    pieces = [
+        Gather(place, buffer, sems[0].at[k], sems[1].at[k]) for k, buffer in enumerate(buffers)
+    ]
+    enter(pieces[0].neighbours())
+    for copy, piece in zip(local, pieces):
+        copy.wait()
+        piece.stage0()
+    for piece in pieces:
+        piece.stage1()
+    for piece in pieces:
+        piece.stage2()
+    for i in ORDER:
+        for piece in pieces:
+            piece.stage3(i)
+    for i in ORDER:
+        for piece in pieces:
+            piece.stage4(i)
+    done = []
+    for k, (piece, out) in enumerate(zip(pieces, outs)):
+        piece.stage5()
+        copy = pltpu.make_async_copy(piece.buffer, out, sems[2].at[k])
+        copy.start()
+        done.append(copy)
+    for copy in done:
+        copy.wait()
+
+
+def gather(qkv_weight, proj_weight, small):
+    widths = (3072, 1024, 128)
+    anyspace = pl.BlockSpec(memory_space=pl.ANY)
+    shapes = [(16, 2, 32, w) for w in widths]
+    outs = pl.pallas_call(
+        gather_kernel,
+        out_shape=[jax.ShapeDtypeStruct(s, BF16) for s in shapes],
+        in_specs=[anyspace] * 3,
+        out_specs=[anyspace] * 3,
+        scratch_shapes=[pltpu.VMEM(s, BF16) for s in shapes]
+        + [
+            pltpu.SemaphoreType.DMA((3, GATHER_SEMS)),
+            pltpu.SemaphoreType.DMA((3, GATHER_SEMS)),
+            pltpu.SemaphoreType.DMA((3,)),
+        ],
+        compiler_params=pltpu.CompilerParams(collective_id=0, has_side_effects=True),
+        name="gather",
+    )(qkv_weight, proj_weight, small)
+    return [o.reshape(D, w) for o, w in zip(outs, widths)]
+
+
+REDUCE_SEMS = 17
+
+
+def reduce_shapes(width):
+    half = width // 2
+    return dict(
+        R=(4, 4, 2, 2, 16, half),
+        A=(4, 4, 4, 16, half),
+        T=(2, 2, 4, 16, half),
+        U=(2, 4, 4, 16, half),
+        B=(4, 4, 16, half),
+        Y=(3, 4, 16, half),
+        C=(4, 16, half),
+        V=(3, 16, half),
+        E=(2, 16, half),
+        Z=(16, half),
+        O=(4, 16, half),
+    )
+
+
+class Reduce:
+    def __init__(self, place, term, width, buffers, send_sems, recv_sems):
+        self.place, self.term, self.half = place, term, width // 2
+        for name, ref in buffers.items():
+            setattr(self, name, ref)
+        self.send_sems, self.recv_sems = send_sems, recv_sems
+        self.sent = []
+
+    def copy(self, src, dst, index, device):
+        return send(src, dst, self.send_sems.at[index], self.recv_sems.at[index], device)
+
+    def start(self, src, dst, index, device):
+        copy = self.copy(src, dst, index, device)
+        copy.start()
+        self.sent.append(copy)
+
+    def arrived(self, ref, index):
+        self.copy(ref, ref, index, self.place.sibling()).wait_recv()
+
+    def finish(self):
+        for copy in self.sent:
+            copy.wait_send()
+
+    def stage0(self):
+        at = self.place
+        self.start(self.term.at[:, :, 1 - at.c], self.R, 0, at.sibling())
+
+    def pair(self, d1):
+        at = self.place
+        for d3 in range(4):
+            chip = at.chip(d3, d1)
+            x, z = chip // 4, chip % 4
+            both = self.term[x, z, at.c].astype(F32) + self.R[x, z].astype(F32)
+            self.A[d1, d3] = both.astype(BF16).reshape(4, 16, self.half)
+
+    def stage1(self):
+        at = self.place
+        self.arrived(self.R, 0)
+        self.pair(2)
+        self.start(self.A.at[2, pl.ds(0, 2)], self.T.at[0], 1, at.along_z(1))
+        self.start(self.A.at[2, pl.ds(2, 2)], self.T.at[1], 2, at.along_z(-1))
+        self.pair(1)
+        self.pair(3)
+        self.pair(0)
+
+    def stage2(self):
+        at = self.place
+        self.arrived(self.T.at[0], 1)
+        self.A[1, 0:2] = (self.A[1, 0:2].astype(F32) + self.T[0].astype(F32)).astype(BF16)
+        self.start(self.A.at[1], self.U.at[0], 3, at.along_z(1))
+        self.arrived(self.T.at[1], 2)
+        self.A[3, 2:4] = (self.A[3, 2:4].astype(F32) + self.T[1].astype(F32)).astype(BF16)
+        self.start(self.A.at[3], self.U.at[1], 4, at.along_z(-1))
+
+    def stage3(self):
+        at = self.place
+        self.arrived(self.U.at[0], 3)
+        self.arrived(self.U.at[1], 4)
+        for d3 in range(4):
+            total = self.A[0, d3].astype(F32) + self.U[0, d3].astype(F32)
+            self.B[d3] = (total + self.U[1, d3].astype(F32)).astype(BF16)
+        for d2 in (2, 1, 3):
+            q = (at.y + d2) % 4
+            self.start(self.B.at[:, q], self.Y.at[d2 - 1], 4 + d2, at.at(dy=d2))
+
+    def stage4(self):
+        at = self.place
+        for d2 in (1, 3, 2):
+            self.arrived(self.Y.at[d2 - 1], 4 + d2)
+        for d3 in (2, 1, 3, 0):
+            total = self.B[d3, at.y].astype(F32) + self.Y[0, d3].astype(F32)
+            total = total + self.Y[1, d3].astype(F32) + self.Y[2, d3].astype(F32)
+            self.C[d3] = total.astype(BF16)
+        low, high = pl.ds(0, 128), pl.ds(128, self.half - 128)
+        self.start(self.C.at[2, :, low], self.V.at[1, :, low], 8, at.along_x(2))
+        self.start(self.C.at[2, :, high], self.V.at[1, :, high], 9, at.along_x(-2))
+        self.start(self.C.at[1], self.V.at[0], 10, at.along_x(1))
+        self.start(self.C.at[3], self.V.at[2], 11, at.along_x(-1))
+
+    def stage5(self):
+        at = self.place
+        low, high = pl.ds(0, 128), pl.ds(128, self.half - 128)
+        self.arrived(self.V.at[0], 10)
+        self.arrived(self.V.at[2], 11)
+        self.arrived(self.V.at[1, :, low], 8)
+        self.arrived(self.V.at[1, :, high], 9)
+        total = self.C[0].astype(F32) + self.V[0].astype(F32)
+        total = total + self.V[1].astype(F32) + self.V[2].astype(F32)
+        self.E[0] = total.astype(BF16)
+        self.start(self.E.at[0], self.Z, 12, at.partner())
+
+    def stage6(self):
+        at = self.place
+        self.arrived(self.Z, 12)
+        total = (self.E[0].astype(F32) + self.Z[...].astype(F32)).astype(BF16)
+        self.E[1] = total
+        for d2 in (2, 1, 3):
+            self.start(self.E.at[1], self.O.at[at.y], 12 + d2, at.at(dy=d2))
+
+    def stage7(self, write):
+        at = self.place
+        for d2 in (1, 3, 2):
+            self.arrived(self.O.at[(at.y - d2 + 4) % 4], 12 + d2)
+        self.O[at.y] = self.E[1]
+        for r in range(2):
+            for k in range(2):
+                write(r, k, self.O[2 * r + k].astype(F32))
+
+    def neighbours(self):
+        at = self.place
+        return (
+            [at.sibling(), at.partner()]
+            + [at.along_z(1), at.along_z(-1)]
+            + [at.along_x(d) for d in (1, -1, 2, -2)]
+            + [at.at(dy=d) for d in (1, 2, 3)]
+        )
+
+
+REDUCE_PIECES = ((0, 0, 768), (0, 768, 768), (0, 1536, 768), (0, 2304, 768), (1, 0, 1024), (2, 0, 512))
+
+
+def reduce_kernel(names, scale, *refs):
+    ins, outs, scratch = refs[:3], refs[3:6], refs[6:]
+    place = Place()
+    per = 1 + len(names)
+    count = len(REDUCE_PIECES)
+    sems = scratch[per * count :]
+    pieces, local = [], []
+    for n, (which, start, width) in enumerate(REDUCE_PIECES):
+        term = scratch[n * per]
+        buffers = dict(zip(names, scratch[n * per + 1 : (n + 1) * per]))
+        pieces.append(Reduce(place, term, width, buffers, sems[0].at[n], sems[1].at[n]))
+        for k in range(2):
+            half = width // 2
+            copy = pltpu.make_async_copy(
+                ins[which].at[:, :, :, :, :, pl.ds(start + k * half, half)],
+                term.at[:, :, :, :, k],
+                sems[2].at[n, k],
+            )
+            copy.start()
+            local.append(copy)
+    enter(pieces[0].neighbours())
+    for n, piece in enumerate(pieces):
+        local[2 * n].wait()
+        local[2 * n + 1].wait()
+        piece.stage0()
+
+    def writer(n):
+        which, start, width = REDUCE_PIECES[n]
+        half = width // 2
+
+        def write(r, k, value):
+            outs[which][r * 16 : r * 16 + 16, start + k * half : start + (k + 1) * half] = (
+                value * scale
+            )
+
+        return write
+
+    for slot in range(count + 6):
+        for n, piece in enumerate(pieces):
+            stage = slot - n + 1
+            if stage == 7:
+                piece.stage7(writer(n))
+            elif 1 <= stage < 7:
+                getattr(piece, f"stage{stage}")()
+    for piece in pieces:
+        piece.finish()
+
+
+def reduce(qkv_term, proj_term, small_term, scale):
+    scratch = []
+    for _, _, width in REDUCE_PIECES:
+        shapes = reduce_shapes(width)
+        scratch.append(pltpu.VMEM((4, 4, 2, 2, 2, 16, width // 2), BF16))
+        scratch += [pltpu.VMEM(s, BF16) for s in shapes.values()]
+    count = len(REDUCE_PIECES)
+    anyspace = pl.BlockSpec(memory_space=pl.ANY)
+    vmem = pl.BlockSpec(memory_space=pltpu.VMEM)
+    widths = (3072, 1024, 512)
+    terms = [
+        t.reshape(4, 4, 2, 2, 16, w) for t, w in zip((qkv_term, proj_term, small_term), widths)
+    ]
+    return pl.pallas_call(
+        functools.partial(reduce_kernel, tuple(shapes), scale),
+        out_shape=[jax.ShapeDtypeStruct((32, w), F32) for w in widths],
+        in_specs=[anyspace] * 3,
+        out_specs=[vmem] * 3,
+        scratch_shapes=scratch
+        + [
+            pltpu.SemaphoreType.DMA((count, REDUCE_SEMS)),
+            pltpu.SemaphoreType.DMA((count, REDUCE_SEMS)),
+            pltpu.SemaphoreType.DMA((count, 2)),
+        ],
+        compiler_params=pltpu.CompilerParams(
+            collective_id=1, has_side_effects=True, vmem_limit_bytes=56 * 2**20
+        ),
+        name="reduce",
+    )(*terms)
 
 
 def block_backward(
@@ -115,9 +504,8 @@
 def per_device(
     tokens, cotangent, patch_count, image_starts, qkv_weight, proj_weight, norm_gain, norm_shift
 ):
-    whole_qkv, whole_proj, whole_gain, whole_shift = side_by_side(
-        (qkv_weight, proj_weight, norm_gain, norm_shift), "fsdp", 0, 1
-    )
+    small = jnp.pad(jnp.stack([norm_gain, norm_shift], axis=1), ((0, 0), (0, 126)))
+    whole_qkv, whole_proj, whole_small = gather(qkv_weight, proj_weight, small)
     grad_block, qkv_term, proj_term, gain_term, shift_term = block_backward(
         tokens,
         cotangent,
@@ -125,42 +513,17 @@
         image_starts[0],
         whole_qkv,
         whole_proj,
-        whole_gain,
-        whole_shift,
+        whole_small[:, 0],
+        whole_small[:, 1],
     )
     replicas = lax.axis_size("dp")
     owners = lax.axis_size("fsdp")
-    factor = 1.0 / math.sqrt(tokens.shape[0] * replicas * owners)
-    terms = (qkv_term, proj_term, gain_term, shift_term)
-    summed = tuple(
-        (
-            part.astype(jnp.float32)
-            for part in sent_together(
-                (
-                    terms[0].astype(jnp.bfloat16),
-                    terms[1].astype(jnp.bfloat16),
-                    terms[2].astype(jnp.bfloat16),
-                    terms[3].astype(jnp.bfloat16),
-                ),
-                "fsdp",
-                0,
-                1,
-            )
-        )
-    )
-    summed = (
-        over_copies(summed[0].astype(jnp.bfloat16), "dp").astype(jnp.float32),
-        over_copies(summed[1].astype(jnp.bfloat16), "dp").astype(jnp.float32),
-        over_copies(summed[2].astype(jnp.bfloat16), "dp").astype(jnp.float32),
-        over_copies(summed[3].astype(jnp.bfloat16), "dp").astype(jnp.float32),
-    )
-    return (
-        grad_block,
-        summed[0] * factor,
-        summed[1] * factor,
-        summed[2] * factor,
-        summed[3] * factor,
-    )
+    scale = 1.0 / math.sqrt(tokens.shape[0] * replicas * owners)
+    small_term = jnp.pad(jnp.stack([gain_term, shift_term], axis=1), ((0, 0), (0, 510)))
+    qkv_grad, proj_grad, small_grad = reduce(
+        qkv_term.astype(BF16), proj_term.astype(BF16), small_term.astype(BF16), scale
+    )
+    return (grad_block, qkv_grad, proj_grad, small_grad[:, 0], small_grad[:, 1])
 
 
 def solution(mesh):

time: 428 us -> 201 us (0.47); the launches traced: 420 us -> 200 us
  waiting for transfers between devices: 268 us -> 0 us
  Pallas kernels: 0 us -> 102 us
  blocking collectives: 17.1 us -> 0 us
  local copies, waits for them, and re-layouts: 26.5 us -> 10.6 us
  between operations: 14.9 us -> 1.43 us
  starting transfers between devices: 11.8 us -> 0 us
  matrix products: 70.3 us -> 79.4 us
  other arithmetic: 11.4 us -> 6.86 us
    reduce_scatter x1 -> x0, waiting for transfers between devices: 158 us -> none  [sent_together(): result = lax.psum_scatter(both, axis, scatter_dimension=dim, tiled=True)]
    pallas_call x0 -> x2, Pallas kernels: none -> 102 us  [the longest x1 66.1 us: reduce(): pl.pallas_call(functools.partial(reduce_kernel, tuple(shapes), scale), ou...]
    all_gather x1 -> x0, waiting for transfers between devices: 66.5 us -> none  [side_by_side(): result, at, done = (lax.all_gather(both, axis, axis=dim, tiled=True), 0, [])]
    all_to_all x3 -> x0, waiting for transfers between devices: 43.2 us -> none  [copy_for_each(): lax.all_to_all(jnp.broadcast_to(shard[None], (size, *shard.shape)), axis,...]
    all_to_all x1 -> x0, blocking collectives: 17.1 us -> none  [copy_for_each(): lax.all_to_all(jnp.broadcast_to(shard[None], (size, *shard.shape)), axis,...]
    concatenate x2 -> x0, local copies, waits for them, and re-layouts: 14.8 us -> none  [the longest x1 13 us: sent_together(): jnp.concatenate([a.reshape(*a.shape[:along], w) for a, w in zip(arrays, w...]
    all_to_all x3 -> x0, starting transfers between devices: 11.7 us -> none  [copy_for_each(): lax.all_to_all(jnp.broadcast_to(shard[None], (size, *shard.shape)), axis,...]
  transfers between devices with their start and end apart: 5 -> 0, of which waited for: 5 -> 0; matrix products, arithmetic and copies ran while one was open for 3% -> 0% of each run, Pallas kernels for 0% -> 0%
where the time goes in v1:
time: 201 us; the launch traced here: 200 us
  Pallas kernels  102 us (51%)
  matrix products  79.4 us (40%)
  local copies, waits for them, and re-layouts  10.6 us (5%)
  other arithmetic  6.86 us (3%)
    pallas_call x1, Pallas kernels, reduce(): pl.pallas_call(functools.partial(reduce_kernel, tuple(shapes), scale), ou...  66.1 us
    pallas_call x1, Pallas kernels, gather(): pl.pallas_call(gather_kernel, out_shape=[jax.ShapeDtypeStruct(s, BF16) fo...  36.1 us
    dot_general x1, matrix products, block_backward(): jnp.einsum('hqk,khe->qhe', grad_scores, keys, preferred_element_type=jnp....  15.6 us
    dot_general x1, matrix products, block_backward(): jnp.einsum('hqk,qhe->khe', grad_scores, queries, preferred_element_type=j...  14.4 us
    dot_general x1, matrix products, block_backward(): jnp.dot(grad_qkv, qkv_weight.T, preferred_element_type=jnp.float32)  7.96 us
    dot_general x1, matrix products, block_backward(): jnp.dot(hidden, qkv_weight, preferred_element_type=jnp.float32)  6.9 us
    dot_general x1, matrix products, block_backward(): jnp.einsum('qhe,khe->hqk', grad_heads, values, preferred_element_type=jnp...  6.23 us
    dot_general x1, matrix products, block_backward(): qkv_term = jnp.dot(hidden.T, grad_qkv, preferred_element_type=jnp.float32)  5.87 us

profile of v1, /device:TPU:32, one launch (start us, length us, event | category | flops | bytes accessed | tf_op | source)
XLA Modules:
  0.0 200.4 jit_solution(10367671828731890111)
XLA Ops:
  0.6 0.0 copy-start
  0.6 1.4 convert_reduce_fusion
  2.0 1.5 fusion.33
  3.5 0.7 pad_maximum_fusion.2
  4.2 0.1 copy.45
  4.3 0.6 pad.9.small_ref
  4.9 36.1 %gather.1 = (bf16[16,2,32,3072]{3,2,1,0:T(8,128)(2,1)}, bf16[16,2,32,1024]{3,2,1,0:T(8,128)(2,1)}, bf16[16,2,32,128]{3,2,1,0:T(8,128)(2,1)}) custom-call(bf16[32,3072]{1,0:T(8,128)(2,1)} %qkv_ref.1, bf16[32,1024]{1,0:T(8,128)(2,1)} %proj_ref.1, bf16[32,128]{1,0:T(8,128)(2,1)} %pad.9.small_ref), custom_call_target="tpu_custom_call" | custom-call | tf_op jit(solution)/shard_map/gather/pallas_call | solution.py:204
  41.0 1.2 slice_convert_fusion.1
  42.2 0.2 copy.62
  42.4 0.2 copy.63
  42.6 0.0 copy-done
  42.6 6.9 %convolution_convert_fusion.1 = bf16[384,3072]{1,0:T(8,128)(2,1)} fusion(bf16[1024,3072]{1,0:T(8,128)(2,1)} %bitcast.87, bf16[384,1024]{1,0:T(8,128)(2,1)S(1)} %copy-done, f32[1024]{0:T(1024)S(1)} %bitcast.84, f32[1024]{0:T(1024)S(1)} %bitcast.80, f32[384]{0:T(512)S(1)} %add_rsqrt_fusion, f32[384]{0:T(512)S(1)} %broadcast_multiply_fusion.2), kind=kOutput, calls=%fused_computation.15 | convolution fusion | flops 2419458048 | bytes 9448448 | tf_op jit(solution)/shard_map/dot_general | solution.py:458
  49.5 3.0 %copy.48 = bf16[384,3072]{0,1:T(8,128)(2,1)S(1)} copy(bf16[384,3072]{1,0:T(8,128)(2,1)} %convolution_convert_fusion.1) | data formatting | bytes 4718592 | tf_op jit(solution)/shard_map/convert_element_type | solution.py:458
  53.1 3.8 %convolution_convert_fusion.3 = bf16[384,1024]{1,0:T(8,128)(2,1)} fusion(bf16[1024,1024]{1,0:T(8,128)(2,1)} %bitcast.89, bf16[384,1024]{1,0:T(8,128)(2,1)} %param.9, pred[384]{0:T(512)(128)(4,1)S(1)} %iota_compare_fusion.1), kind=kOutput, calls=%fused_computation.43 | convolution fusion | flops 806092800 | bytes 3670400 | tf_op jit(solution)/shard_map/dot_general | solution.py:476
  56.9 2.3 %copy.49 = bf16[384,1024]{0,1:T(8,128)(2,1)} copy(bf16[384,1024]{1,0:T(8,128)(2,1)} %convolution_convert_fusion.3) | data formatting | bytes 1572864 | tf_op jit(solution)/shard_map/convert_element_type | solution.py:476
  59.2 0.0 copy-start.9
  59.2 6.2 %fusion.57 = f32[16,384,384]{1,2,0:T(8,128)} fusion(bf16[384,16,64]{0,2,1:T(8,128)(2,1)} %bitcast.74, bf16[384,3,16,64]{0,3,2,1:T(8,128)(2,1)S(1)} %bitcast.69), kind=kOutput, calls=%fused_computation.53 | convolution fusion | flops 301989888 | bytes 11010048 | tf_op jit(solution)/shard_map/qhe,khe->hqk/dot_general | solution.py:480
  65.5 0.0 copy-done.9
  65.5 0.1 convert_reduce_fusion.1
  65.5 0.2 compare_and_fusion
  65.7 5.6 %fusion.69 = (f32[16,384]{1,0:T(8,128)S(1)}, f32[16,384,384]{1,2,0:T(8,128)}) fusion(pred[384,384]{0,1:T(8,128)(4,1)S(1)} %compare_and_fusion, bf16[384,3,16,64]{0,3,2,1:T(8,128)(2,1)S(1)} %bitcast.70), kind=kOutput, calls=%fused_computation.77 | convolution fusion | flops 311427456 | bytes 11182080 | tf_op jit(solution)/shard_map/sub | solution.py:466
  71.3 15.6 %fusion.49 = bf16[384,1,16,64]{0,3,2,1:T(8,128)(2,1)} fusion(f32[16,384,384]{1,2,0:T(8,128)} %fusion.57, bf16[384,3,16,64]{0,3,2,1:T(8,128)(2,1)S(1)} %bitcast.71, f32[16,384,384]{1,2,0:T(8,128)} %get-tuple-element.26, f32[16,384]{1,0:T(8,128)S(1)} %get-tuple-element.25), kind=kOutput, calls=%fused_computation.46 | convolution fusion | flops 318904704 | bytes 39370752 | tf_op jit(solution)/shard_map/hqk,khe->qhe/dot_general | solution.py:486
  86.9 14.4 %fusion.46 = bf16[384,1,16,64]{0,3,2,1:T(8,128)(2,1)} fusion(f32[16,384,384]{1,2,0:T(8,128)} %fusion.57, bf16[384,3,16,64]{0,3,2,1:T(8,128)(2,1)S(1)} %bitcast.72, f32[16,384,384]{1,2,0:T(8,128)} %get-tuple-element.26, f32[16,384]{1,0:T(8,128)S(1)} %get-tuple-element.25), kind=kOutput, calls=%fused_computation.45 | convolution fusion | flops 318904704 | bytes 39370752 | tf_op jit(solution)/shard_map/hqk,qhe->khe/dot_general | solution.py:489
  101.3 0.0 copy-start.4
  101.3 0.0 copy-start.5
  101.3 5.8 %fusion.52 = bf16[384,1,16,64]{0,3,2,1:T(8,128)(2,1)S(1)} fusion(bf16[384,16,64]{0,2,1:T(8,128)(2,1)} %bitcast.75, f32[16,384,384]{1,2,0:T(8,128)} %get-tuple-element.26, f32[16,384]{1,0:T(8,128)S(1)} %get-tuple-element.25), kind=kOutput, calls=%fused_computation.47 | convolution fusion | flops 307101696 | bytes 11034624 | tf_op jit(solution)/shard_map/hqk,qhe->khe/dot_general | solution.py:481
  107.1 0.0 copy-done.4
  107.1 0.0 copy-done.5
  107.1 0.3 pad_maximum_fusion
  107.5 0.0 copy-start.1
  107.5 8.0 %fusion.32 = (bf16[1024]{0:T(1024)(128)(2,1)S(1)}, f32[384]{0:T(512)S(1)}, f32[384]{0:T(512)S(1)}, bf16[1024]{0:T(1024)(128)(2,1)S(1)}, f32[384,1024]{1,0:T(8,128)}) fusion(bf16[384,1024]{1,0:T(8,128)(2,1)S(1)} %copy-done, f32[384]{0:T(512)S(1)} %add_rsqrt_fusion, f32[384]{0:T(512)S(1)} %broadcast_multiply_fusion.2, f32[1024]{0:T(1024)S(1)} %bitcast.81, ...), kind=kOutput, calls=%fused_computation.37 | convolution fusion | flops 2419848192 | bytes 11024384 | tf_op jit(solution)/shard_map/dot_general | solution.py:494
  115.4 0.0 copy-done.1
  115.5 0.2 copy.61
  115.7 1.1 pad.10.clone
  116.7 0.0 copy-start.6
  116.8 4.6 %fusion.37 = bf16[16,64,384]{2,1,0:T(8,128)(2,1)S(1)} fusion(bf16[384,3,16,64]{0,3,2,1:T(8,128)(2,1)S(1)} %bitcast.73, f32[16,384,384]{1,2,0:T(8,128)} %get-tuple-element.26, f32[16,384]{1,0:T(8,128)S(1)} %get-tuple-element.25), kind=kOutput, calls=%fused_computation.40 | convolution fusion | flops 307101696 | bytes 11034624 | tf_op jit(solution)/shard_map/hqk,khe->qhe/dot_general | solution.py:470
  121.4 0.0 copy-start.2
  121.4 0.0 copy-done.6
  121.4 2.7 %convolution_convert_fusion.2 = bf16[1024,1024]{1,0:T(8,128)(2,1)} fusion(bf16[384,1024]{0,1:T(8,128)(2,1)S(1)} %bitcast.92, bf16[384,1024]{1,0:T(8,128)(2,1)S(1)} %copy-done.6, pred[384]{0:T(512)(128)(4,1)S(1)} %iota_compare_fusion.1), kind=kOutput, calls=%fused_computation.23 | convolution fusion | flops 806748160 | bytes 3670400 | tf_op jit(solution)/shard_map/dot_general | solution.py:475
  124.1 0.0 copy-done.2
  124.1 5.9 %convolution_convert_fusion = bf16[1024,3072]{1,0:T(8,128)(2,1)} fusion(bf16[384,3072]{0,1:T(8,128)(2,1)S(1)} %bitcast.77, bf16[384,1024]{1,0:T(8,128)(2,1)S(1)} %copy-done, f32[1024]{0:T(1024)S(1)} %bitcast.85, f32[1024]{0:T(1024)S(1)} %bitcast.82, f32[384]{0:T(512)S(1)} %add_rsqrt_fusion, f32[384]{0:T(512)S(1)} %broadcast_multiply_fusion.2), kind=kOutput, calls=%fused_computation.8 | convolution fusion | flops 2421424128 | bytes 9448448 | tf_op jit(solution)/shard_map/dot_general | solution.py:493
  129.9 0.0 copy-start.3
  129.9 66.1 %reduce.5 = (f32[32,3072]{1,0:T(8,128)}, f32[32,1024]{1,0:T(8,128)}, f32[32,512]{1,0:T(8,128)}) custom-call(bf16[4,4,2,2,16,3072]{5,4,3,2,1,0:T(8,128)(2,1)} %bitcast.67, bf16[4,4,2,2,16,1024]{5,4,3,2,1,0:T(8,128)(2,1)} %bitcast.78, bf16[4,4,2,2,16,512]{5,4,3,2,1,0:T(8,128)(2,1)} %bitcast.68), custom_call_target="tpu_custom_call" | custom-call | tf_op jit(solution)/shard_map/reduce/pallas_call | solution.py:423
  196.0 0.0 copy-start.7
  196.0 1.5 slice_reduce_fusion
  197.5 0.0 copy-done.3
  197.5 0.0 copy-start.8
  197.5 1.5 fusion.31
  199.0 0.0 copy-done.7
  199.0 0.7 copy.67
  199.8 0.0 copy-done.8
  199.8 0.7 copy.68
  (7 shorter events, 0.0 us)
Async XLA Ops:
  0.6 41.9 %copy-start = (bf16[384,1024]{1,0:T(8,128)(2,1)S(1)}, bf16[384,1024]{1,0:T(8,128)(2,1)}, u32[]{:S(2)}) copy-start(bf16[384,1024]{1,0:T(8,128)(2,1)} %param.8) | copy-start | bytes 2359300
  59.2 6.2 %copy-start.9 = (s32[1,8]{1,0:T(1,128)S(1)}, s32[1,8]{1,0:T(1,128)}, u32[]{:S(2)}) copy-start(s32[1,8]{1,0:T(1,128)} %param.11) | copy-start | bytes 100
  101.3 5.8 %copy-start.4 = (bf16[384,1,16,64]{0,3,2,1:T(8,128)(2,1)S(1)}, bf16[384,1,16,64]{0,3,2,1:T(8,128)(2,1)}, u32[]{:S(2)}) copy-start(bf16[384,1,16,64]{0,3,2,1:T(8,128)(2,1)} %fusion.49) | copy-start | bytes 2359300
  101.3 5.8 %copy-start.5 = (bf16[384,1,16,64]{0,3,2,1:T(8,128)(2,1)S(1)}, bf16[384,1,16,64]{0,3,2,1:T(8,128)(2,1)}, u32[]{:S(2)}) copy-start(bf16[384,1,16,64]{0,3,2,1:T(8,128)(2,1)} %fusion.46) | copy-start | bytes 2359300
  107.5 8.0 %copy-start.1 = (bf16[384,3,16,64]{0,3,2,1:T(8,128)(2,1)}, bf16[384,3,16,64]{0,3,2,1:T(8,128)(2,1)S(1)}, u32[]{:S(2)}) copy-start(bf16[384,3,16,64]{0,3,2,1:T(8,128)(2,1)S(1)} %pad_maximum_fusion) | copy-start | bytes 7077892
  116.7 4.6 %copy-start.6 = (bf16[384,1024]{1,0:T(8,128)(2,1)S(1)}, bf16[384,1024]{1,0:T(8,128)(2,1)}, u32[]{:S(2)}) copy-start(bf16[384,1024]{1,0:T(8,128)(2,1)} %param.9) | copy-start | bytes 2359300
  121.4 2.7 %copy-start.2 = (bf16[384,3,16,64]{0,3,2,1:T(8,128)(2,1)S(1)}, bf16[384,3,16,64]{0,3,2,1:T(8,128)(2,1)}, u32[]{:S(2)}) copy-start(bf16[384,3,16,64]{0,3,2,1:T(8,128)(2,1)} %copy-done.1) | copy-start | bytes 7077892
  129.9 67.6 %copy-start.3 = (f32[384,1024]{1,0:T(8,128)S(1)}, f32[384,1024]{1,0:T(8,128)}, u32[]{:S(2)}) copy-start(f32[384,1024]{1,0:T(8,128)} %get-tuple-element.27) | copy-start | bytes 4718596
  196.0 3.0 %copy-start.7 = (f32[32,3072]{1,0:T(8,128)S(1)}, f32[32,3072]{1,0:T(8,128)}, u32[]{:S(2)}) copy-start(f32[32,3072]{1,0:T(8,128)} %get-tuple-element.36) | copy-start | bytes 1179652
  197.5 2.3 %copy-start.8 = (f32[32,1024]{1,0:T(8,128)S(1)}, f32[32,1024]{1,0:T(8,128)}, u32[]{:S(2)}) copy-start(f32[32,1024]{1,0:T(8,128)} %get-tuple-element.37) | copy-start | bytes 393220

commit v2 on v0

v2 whole, which is shorter than its diff:
```python
import functools
import math

import jax
import jax.numpy as jnp
from jax import lax
from jax.experimental import pallas as pl
from jax.experimental.pallas import tpu as pltpu
from jax.sharding import PartitionSpec as P

MESH = pl.DeviceIdType.MESH
F32 = jnp.float32
BF16 = jnp.bfloat16
D = 1024
ROWS = 384


def nn(a, b):
    return lax.dot_general(a, b, (((1,), (0,)), ((), ())), preferred_element_type=F32)


def nt(a, b):
    return lax.dot_general(a, b, (((1,), (1,)), ((), ())), preferred_element_type=F32)


def tn(a, b):
    return lax.dot_general(a, b, (((0,), (0,)), ((), ())), preferred_element_type=F32)


class Place:
    def __init__(self):
        dp, fsdp = lax.axis_index("dp"), lax.axis_index("fsdp")
        self.y, self.zhi = dp // 2, dp % 2
        self.c = fsdp % 2
        chip = fsdp // 2
        self.x, self.zlo = chip // 4, chip % 4
        self.z = self.zhi * 4 + self.zlo

    def at(self, dx=0, dy=0, dz=0, flip=0):
        x = (self.x + dx + 4) % 4
        y = (self.y + dy + 4) % 4
        z = (self.z + dz + 8) % 8
        c = self.c + flip * (1 - 2 * self.c)
        return {"dp": y * 2 + z // 4, "fsdp": (x * 4 + z % 4) * 2 + c}

    def along_x(self, d):
        return self.at(dx=(1 - self.c) * d, dz=self.c * d)

    def along_z(self, d):
        return self.at(dx=self.c * d, dz=(1 - self.c) * d)

    def chip(self, i, j):
        x = (self.x + (1 - self.c) * i + self.c * j + 8) % 4
        z = (self.zlo + self.c * i + (1 - self.c) * j + 8) % 4
        return x, z

    def sibling(self):
        return self.at(flip=1)

    def partner(self):
        return self.at(dz=4)

    def all(self):
        return (
            [self.sibling(), self.partner()]
            + [self.along_z(1), self.along_z(-1)]
            + [self.along_x(d) for d in (1, -1, 2, -2)]
            + [self.at(dy=d) for d in (1, 2, 3)]
        )


def enter(devices):
    barrier = pltpu.get_barrier_semaphore()
    for device in devices:
        pl.semaphore_signal(barrier, inc=1, device_id=device, device_id_type=MESH)
    pl.semaphore_wait(barrier, len(devices))


class Copies:
    def __init__(self, place, send_sems, recv_sems):
        self.place, self.send_sems, self.recv_sems = place, send_sems, recv_sems

    def copy(self, src, dst, n, device):
        return pltpu.make_async_remote_copy(
            src_ref=src,
            dst_ref=dst,
            send_sem=self.send_sems.at[n],
            recv_sem=self.recv_sems.at[n],
            device_id=device,
            device_id_type=MESH,
        )

    def start(self, src, dst, n, device):
        self.copy(src, dst, n, device).start()

    def arrived(self, ref, n):
        self.copy(ref, ref, n, self.place.sibling()).wait_recv()

    def left(self, ref, n):
        self.copy(ref, ref, n, self.place.sibling()).wait_send()


GATHER_SEMS = 36
ORDER = (0, -1, 1, 2)


class Gather(Copies):
    def __init__(self, place, buffer, send_sems, recv_sems):
        super().__init__(place, send_sems, recv_sems)
        self.buffer = buffer

    def block(self, i, j, half=None):
        x, z = self.place.chip(i, j)
        ref = self.buffer.at[x, z, self.place.c]
        return ref if half is None else ref.at[pl.ds(half * 16, 16)]

    def forward(self, ref, n, device):
        self.start(ref, ref, n, device)

    def to_second(self, i):
        self.forward(self.block(i, 0), 4 + 4 * (i % 4), self.place.along_z(1))
        self.forward(self.block(i, 0), 5 + 4 * (i % 4), self.place.along_z(-1))
        self.to_sibling(i, 0)

    def to_sibling(self, i, j):
        self.forward(self.block(i, j), 20 + 4 * (i % 4) + (j % 4), self.place.sibling())

    def stage0(self):
        self.forward(self.block(0, 0), 0, self.place.along_x(1))
        self.forward(self.block(0, 0), 1, self.place.along_x(-1))
        self.to_second(0)

    def stage1(self):
        self.arrived(self.block(-1, 0), 0)
        self.forward(self.block(-1, 0, 0), 2, self.place.along_x(1))
        self.arrived(self.block(1, 0), 1)
        self.forward(self.block(1, 0, 1), 3, self.place.along_x(-1))
        self.to_second(-1)
        self.to_second(1)

    def stage2(self):
        self.arrived(self.block(2, 0, 0), 2)
        self.arrived(self.block(2, 0, 1), 3)
        self.to_second(2)

    def stage3(self):
        for i in ORDER:
            k = i % 4
            self.arrived(self.block(i, -1), 4 + 4 * k)
            self.forward(self.block(i, -1, 0), 6 + 4 * k, self.place.along_z(1))
            self.to_sibling(i, -1)
            self.arrived(self.block(i, 1), 5 + 4 * k)
            self.forward(self.block(i, 1, 1), 7 + 4 * k, self.place.along_z(-1))
            self.to_sibling(i, 1)

    def stage4(self):
        for i in ORDER:
            k = i % 4
            self.arrived(self.block(i, 2, 0), 6 + 4 * k)
            self.arrived(self.block(i, 2, 1), 7 + 4 * k)
            self.to_sibling(i, 2)

    def stage5(self):
        for i in range(4):
            for j in range(4):
                x, z = self.place.chip(j, i)
                self.arrived(self.buffer.at[x, z, 1 - self.place.c], 20 + 4 * i + j)

    def drain(self):
        whole, half = self.block(0, 0), self.block(0, 0, 0)
        for n in range(GATHER_SEMS):
            self.left(half if n in (2, 3) or (n < 20 and n % 4 > 1) else whole, n)


REDUCE_SEMS = 16


def reduce_shapes(width):
    half = width // 2
    return dict(
        R=(4, 4, 2, 2, 16, half),
        A=(4, 4, 4, 16, half),
        T=(2, 2, 4, 16, half),
        U=(2, 4, 4, 16, half),
        B=(4, 4, 16, half),
        Y=(3, 4, 16, half),
        C=(4, 16, half),
        V=(3, 16, half),
        E=(2, 16, half),
        Z=(16, half),
        O=(4, 16, half),
    )


REDUCE_NAMES = tuple(reduce_shapes(256))


class Reduce(Copies):
    def __init__(self, place, term, buffers, half, send_sems, recv_sems):
        super().__init__(place, send_sems, recv_sems)
        self.term, self.half = term, half
        for name, ref in zip(REDUCE_NAMES, buffers):
            setattr(self, name, ref)
        self.low, self.high = pl.ds(0, 128), pl.ds(128, half - 128)

    def stage0(self):
        self.start(self.term.at[:, :, 1 - self.place.c], self.R, 0, self.place.sibling())

    def pair(self, d1):
        for d3 in range(4):
            x, z = self.place.chip(d3, d1)
            both = self.term[x, z, self.place.c].astype(F32) + self.R[x, z].astype(F32)
            self.A[d1, d3] = both.astype(BF16).reshape(4, 16, self.half)

    def stage1(self):
        self.arrived(self.R, 0)
        self.pair(2)
        self.start(self.A.at[2, pl.ds(0, 2)], self.T.at[0], 1, self.place.along_z(1))
        self.start(self.A.at[2, pl.ds(2, 2)], self.T.at[1], 2, self.place.along_z(-1))
        self.pair(1)
        self.pair(3)
        self.pair(0)

    def stage2(self):
        self.arrived(self.T.at[0], 1)
        self.A[1, 0:2] = (self.A[1, 0:2].astype(F32) + self.T[0].astype(F32)).astype(BF16)
        self.start(self.A.at[1], self.U.at[0], 3, self.place.along_z(1))
        self.arrived(self.T.at[1], 2)
        self.A[3, 2:4] = (self.A[3, 2:4].astype(F32) + self.T[1].astype(F32)).astype(BF16)
        self.start(self.A.at[3], self.U.at[1], 4, self.place.along_z(-1))

    def stage3(self):
        self.arrived(self.U.at[0], 3)
        self.arrived(self.U.at[1], 4)
        for d3 in range(4):
            total = self.A[0, d3].astype(F32) + self.U[0, d3].astype(F32)
            self.B[d3] = (total + self.U[1, d3].astype(F32)).astype(BF16)
        for d2 in (2, 1, 3):
            q = (self.place.y + d2) % 4
            self.start(self.B.at[:, q], self.Y.at[d2 - 1], 4 + d2, self.place.at(dy=d2))

    def stage4(self):
        for d2 in (1, 3, 2):
            self.arrived(self.Y.at[d2 - 1], 4 + d2)
        for d3 in range(4):
            total = self.B[d3, self.place.y].astype(F32) + self.Y[0, d3].astype(F32)
            total = total + self.Y[1, d3].astype(F32) + self.Y[2, d3].astype(F32)
            self.C[d3] = total.astype(BF16)
        low, high = self.low, self.high
        self.start(self.C.at[2, :, low], self.V.at[1, :, low], 8, self.place.along_x(2))
        self.start(self.C.at[2, :, high], self.V.at[1, :, high], 9, self.place.along_x(-2))
        self.start(self.C.at[1], self.V.at[0], 10, self.place.along_x(1))
        self.start(self.C.at[3], self.V.at[2], 11, self.place.along_x(-1))

    def stage5(self):
        self.arrived(self.V.at[0], 10)
        self.arrived(self.V.at[2], 11)
        self.arrived(self.V.at[1, :, self.low], 8)
        self.arrived(self.V.at[1, :, self.high], 9)
        total = self.C[0].astype(F32) + self.V[0].astype(F32)
        total = total + self.V[1].astype(F32) + self.V[2].astype(F32)
        self.E[0] = total.astype(BF16)
        self.start(self.E.at[0], self.Z, 12, self.place.partner())

    def stage6(self):
        self.arrived(self.Z, 12)
        self.E[1] = (self.E[0].astype(F32) + self.Z[...].astype(F32)).astype(BF16)
        for d2 in (2, 1, 3):
            self.start(self.E.at[1], self.O.at[self.place.y], 12 + d2, self.place.at(dy=d2))

    def stage7(self, write):
        for d2 in (1, 3, 2):
            self.arrived(self.O.at[(self.place.y - d2 + 4) % 4], 12 + d2)
        self.O[self.place.y] = self.E[1]
        for r in range(2):
            for k in range(2):
                write(r, k, self.O[2 * r + k].astype(F32))

    def drain(self):
        self.left(self.R, 0)
        self.left(self.T.at[0], 1)
        self.left(self.T.at[1], 2)
        self.left(self.U.at[0], 3)
        self.left(self.U.at[1], 4)
        for d2 in (1, 2, 3):
            self.left(self.Y.at[d2 - 1], 4 + d2)
            self.left(self.Z, 12 + d2)
        self.left(self.V.at[1, :, self.low], 8)
        self.left(self.V.at[1, :, self.high], 9)
        self.left(self.V.at[0], 10)
        self.left(self.V.at[2], 11)
        self.left(self.Z, 12)


SCRATCH = {
    "normed": ((384, 1024), F32),
    "inverse": ((384, 128), F32),
    "hidden": ((384, 1024), BF16),
    "hidden_t": ((1024, 384), BF16),
    "mcot": ((384, 1024), BF16),
    "live": ((384, 128), F32),
    "ga": ((4, 384, 256), BF16),
    "att": ((4, 384, 256), BF16),
    "qkv": ((384, 768), BF16),
    "dqkv": ((4, 384, 768), BF16),
    "bias": ((384, 384), F32),
    "gains": ((2, 1024), F32),
    "probs": ((2, 384, 384), BF16),
    "dscores": ((2, 384, 384), BF16),
    "gh": ((384, 1024), F32),
}


def prologue_tokens(S, tok_ref, count_ref, starts_ref):
    source = tok_ref[...].astype(F32)
    center = jnp.mean(source, axis=1, keepdims=True)
    centered = source - center
    variance = jnp.mean(centered * centered, axis=1, keepdims=True)
    inverse = lax.rsqrt(variance + 1e-06)
    S["normed"][...] = centered * inverse
    S["inverse"][...] = jnp.broadcast_to(inverse, (ROWS, 128))
    count = count_ref[0]
    down = lax.broadcasted_iota(jnp.int32, (ROWS, 1), 0)
    across = lax.broadcasted_iota(jnp.int32, (1, ROWS), 1)
    seg_down = jnp.zeros((ROWS, 1), jnp.int32)
    seg_across = jnp.zeros((1, ROWS), jnp.int32)
    for j in range(8):
        start = starts_ref[0, j]
        seg_down = seg_down + jnp.where(down >= start, 1, 0)
        seg_across = seg_across + jnp.where(across >= start, 1, 0)
    seg_down = jnp.where(down < count, seg_down, -1)
    seg_across = jnp.where(across < count, seg_across, -2)
    S["bias"][...] = jnp.where(seg_down == seg_across, 0.0, -1e30).astype(F32)
    alive = lax.broadcasted_iota(jnp.int32, (ROWS, 128), 0) < count
    S["live"][...] = jnp.where(alive, 1.0, 0.0).astype(F32)


def prologue_weights(S, tok_ref, cot_ref):
    weights = S["Wps"]
    small = weights[:, :, :, :, 1024:1152].reshape(1024, 128).astype(F32)
    S["gains"][...] = small.T[0:2, :]
    gain = S["gains"][0:1, :]
    shift = S["gains"][1:2, :]
    S["hidden"][...] = (S["normed"][...] * gain + shift).astype(BF16)
    S["hidden_t"][...] = S["hidden"][...].T
    cot = cot_ref[...]
    alive = S["live"][:, 0:1] > 0.5
    S["mcot"][...] = jnp.where(alive, cot.astype(F32), 0.0).astype(BF16)
    for g in range(4):
        part = weights[g, :, :, :, 0:1024].reshape(256, 1024)
        S["ga"][g] = nt(S["mcot"][...], part).astype(BF16)


def group(S, g, hook):
    weight = S["Wg"][g].reshape(1024, 768)
    for n in range(3):
        part = nn(S["hidden"][...], S["Wg"][g, :, :, :, :, n * 256 : n * 256 + 256].reshape(1024, 256))
        part = part.astype(BF16)
        S["qkv"][:, n * 256 : n * 256 + 256] = part * jnp.asarray(0.125, BF16) if n == 0 else part
    lane = lax.broadcasted_iota(jnp.int32, (ROWS, 128), 1)
    first = lane < 64
    for pair in range(2):
        q2 = S["qkv"][:, pair * 128 : pair * 128 + 128]
        k2 = S["qkv"][:, 256 + pair * 128 : 384 + pair * 128]
        v2 = S["qkv"][:, 512 + pair * 128 : 640 + pair * 128]
        o2 = S["ga"][g, :, pair * 128 : pair * 128 + 128]
        zero = jnp.zeros_like(q2)

        def own(a, h):
            return jnp.where(first, a, zero) if h == 0 else jnp.where(first, zero, a)

        for h in range(2):
            hook(2 * pair + h)
            scores = nt(own(q2, h), k2) + S["bias"][...]
            row_max = jnp.max(scores, axis=1, keepdims=True)
            expon = jnp.exp(scores - row_max)
            probs = expon * (1.0 / jnp.sum(expon, axis=1, keepdims=True))
            S["probs"][h] = probs.astype(BF16)
            grad_probs = nt(own(o2, h), v2)
            delta = jnp.sum(probs * grad_probs, axis=1, keepdims=True)
            S["dscores"][h] = (probs * (grad_probs - delta)).astype(BF16)
        att = sum(nn(S["probs"][h], own(v2, h)) for h in range(2))
        S["att"][g, :, pair * 128 : pair * 128 + 128] = att.astype(BF16)
        dv = sum(tn(S["probs"][h], own(o2, h)) for h in range(2))
        dq = sum(nn(S["dscores"][h], own(k2, h)) for h in range(2)) * 0.125
        dk = sum(tn(S["dscores"][h], own(q2, h)) for h in range(2))
        S["dqkv"][g, :, pair * 128 : pair * 128 + 128] = dq.astype(BF16)
        S["dqkv"][g, :, 256 + pair * 128 : 384 + pair * 128] = dk.astype(BF16)
        S["dqkv"][g, :, 512 + pair * 128 : 640 + pair * 128] = dv.astype(BF16)
    hook(4)
    for m in range(4):
        part = nn(S["hidden_t"][m * 256 : m * 256 + 256], S["dqkv"][g]).astype(BF16)
        part = part.reshape(4, 2, 2, 16, 768)
        for k in range(2):
            S["G"][g, m, :, :, :, k] = part[..., k * 384 : k * 384 + 384]
    hook(5)


def proj_grads(S):
    for g in range(4):
        part = tn(S["att"][g], S["mcot"][...]).astype(BF16).reshape(4, 2, 2, 16, 1024)
        for k in range(2):
            S["Gp"][g, :, :, :, k] = part[..., k * 512 : k * 512 + 512]


def grads_hidden(S, between):
    for n in range(4):
        S["gh"][:, n * 256 : n * 256 + 256] = sum(
            nt(S["dqkv"][g], S["Wg"][g, n].reshape(256, 768)) for g in range(4)
        )
        between(n)


def small_grads(S):
    gh = S["gh"][...]
    gain_term = jnp.sum(gh * S["normed"][...], axis=0, keepdims=True)
    shift_term = jnp.sum(gh, axis=0, keepdims=True)
    rows = lax.broadcasted_iota(jnp.int32, (128, 1024), 0)
    both = jnp.where(rows == 0, gain_term, jnp.where(rows == 1, shift_term, 0.0))
    columns = both.T.astype(BF16).reshape(4, 4, 2, 2, 16, 128)
    zero = jnp.zeros_like(columns)
    S["Gs"][:, :, :, :, 0, :, 0:128] = columns
    S["Gs"][:, :, :, :, 0, :, 128:256] = zero
    S["Gs"][:, :, :, :, 1, :, 0:128] = zero
    S["Gs"][:, :, :, :, 1, :, 128:256] = zero


def token_grads(S, cot_ref, out_ref):
    normed = S["normed"][...]
    grad_normed = S["gh"][...] * S["gains"][0:1, :]
    inner = grad_normed - jnp.mean(grad_normed, axis=1, keepdims=True)
    inner = inner - normed * jnp.mean(grad_normed * normed, axis=1, keepdims=True)
    out_ref[...] = (cot_ref[...].astype(F32) + S["inverse"][:, 0:1] * inner).astype(BF16)


COMM = {}
for _name, _shape in reduce_shapes(768).items():
    COMM["g_" + _name] = ((4,) + _shape, BF16)
for _name, _shape in reduce_shapes(1024).items():
    COMM["p_" + _name] = (_shape, BF16)
for _name, _shape in reduce_shapes(512).items():
    COMM["s_" + _name] = (_shape, BF16)
COMM["Wg"] = ((4, 4, 4, 2, 32, 768), BF16)
COMM["Wps"] = ((4, 4, 2, 32, 1152), BF16)
COMM["G"] = ((4, 4, 4, 2, 2, 2, 16, 384), BF16)
COMM["Gp"] = ((4, 4, 2, 2, 2, 16, 512), BF16)
COMM["Gs"] = ((4, 4, 2, 2, 2, 16, 256), BF16)


def kernel(
    scale,
    count_ref,
    starts_ref,
    tok_ref,
    cot_ref,
    qkv_ref,
    proj_ref,
    small_ref,
    out_ref,
    qkv_out,
    proj_out,
    small_out,
    *scratch,
):
    S = dict(zip(tuple(SCRATCH) + tuple(COMM), scratch))
    gs, gr, rs, rr, ls = scratch[len(S) :]
    place = Place()
    x, z, c = place.x, place.zlo, place.c

    local = []
    for n, (src, dst) in enumerate(
        [
            (proj_ref, S["Wps"].at[x, z, c, :, pl.ds(0, 1024)]),
            (small_ref, S["Wps"].at[x, z, c, :, pl.ds(1024, 128)]),
        ]
        + [
            (
                qkv_ref.at[:, pl.ds(part * 1024 + g * 256, 256)],
                S["Wg"].at[g, x, z, c, :, pl.ds(part * 256, 256)],
            )
            for g in range(4)
            for part in range(3)
        ]
    ):
        copy = pltpu.make_async_copy(src, dst, ls.at[n])
        copy.start()
        local.append(copy)

    def piece(k):
        if isinstance(k, int) and k == 0:
            return Gather(place, S["Wps"], gs.at[0], gr.at[0])
        return Gather(place, S["Wg"].at[k - 1], gs.at[k], gr.at[k])

    def term(k):
        buffers = [S["g_" + name].at[k] for name in REDUCE_NAMES]
        return Reduce(place, S["G"].at[k], buffers, 384, rs.at[k], rr.at[k])

    def write_group(g):
        def write(r, k, value):
            value = value * scale
            rows = pl.ds(r * 16, 16)

            def at(first, width):
                return pl.ds(pl.multiple_of(first + g * 256, 128), width)

            if k == 0:
                qkv_out[rows, at(0, 256)] = value[:, 0:256]
                qkv_out[rows, at(1024, 128)] = value[:, 256:384]
            else:
                qkv_out[rows, at(1152, 128)] = value[:, 0:128]
                qkv_out[rows, at(2048, 256)] = value[:, 128:384]

        return write

    def write_to(ref, half):
        def write(r, k, value):
            ref[r * 16 : r * 16 + 16, k * half : (k + 1) * half] = value * scale

        return write

    enter(place.all())
    for copy in local:
        copy.wait()
    for k in range(3):
        piece(k).stage0()
    prologue_tokens(S, tok_ref, count_ref, starts_ref)
    piece(0).stage1()
    piece(1).stage1()
    piece(0).stage2()
    piece(1).stage2()
    piece(2).stage1()
    piece(0).stage3()
    piece(3).stage0()
    piece(1).stage3()
    piece(2).stage2()
    piece(0).stage4()
    piece(1).stage4()
    piece(3).stage1()
    piece(0).stage5()
    prologue_weights(S, tok_ref, cot_ref)
    piece(2).stage3()
    piece(1).stage5()

    def body(g, carry):
        def hook(k):
            gathers = {
                0: ((2, "stage4"), (3, "stage2")),
                1: ((4, "stage0"),),
                2: ((3, "stage3"),),
                3: ((4, "stage1"),),
                4: ((2, "stage5"),),
            }
            for ahead, stage in gathers.get(k, ()):

                @pl.when(g + ahead <= 4)
                def _():
                    getattr(piece(g + ahead), stage)()

            reduces = {
                0: ((2, "stage4"),),
                1: ((1, "stage1"),),
                2: ((2, "stage5"),),
                3: ((1, "stage2"),),
                4: ((2, "stage6"),),
                5: ((1, "stage3"), (2, "stage7"), (0, "stage0")),
            }
            for behind, stage in reduces.get(k, ()):

                @pl.when(g >= behind)
                def _():
                    if stage == "stage7":
                        term(g - behind).stage7(write_group(g - behind))
                    else:
                        getattr(term(g - behind), stage)()

        group(S, g, hook)
        return carry

    lax.fori_loop(0, 4, body, 0)

    proj = Reduce(
        place, S["Gp"], [S["p_" + n] for n in REDUCE_NAMES], 512, rs.at[4], rr.at[4]
    )
    small = Reduce(
        place, S["Gs"], [S["s_" + n] for n in REDUCE_NAMES], 256, rs.at[5], rr.at[5]
    )
    proj_grads(S)
    proj.stage0()
    term(3).stage1()
    term(2).stage4()

    def between(n):
        if n == 0:
            proj.stage1()
        elif n == 1:
            term(3).stage2()
            term(2).stage5()
        elif n == 2:
            proj.stage2()
        else:
            term(3).stage3()

    grads_hidden(S, between)
    small_grads(S)
    small.stage0()
    term(2).stage6()
    proj.stage3()
    small.stage1()
    token_grads(S, cot_ref, out_ref)
    term(3).stage4()
    small.stage2()
    proj.stage4()
    term(3).stage5()
    small.stage3()
    term(2).stage7(write_group(2))
    proj.stage5()
    term(3).stage6()
    small.stage4()
    proj.stage6()
    small.stage5()
    term(3).stage7(write_group(3))
    small.stage6()
    proj.stage7(write_to(proj_out, 512))
    small.stage7(write_to(small_out, 256))

    piece(0).drain()

    def drain(k, carry):
        piece(k + 1).drain()
        term(k).drain()
        return carry

    lax.fori_loop(0, 4, drain, 0)
    proj.drain()
    small.drain()


def fused(counts, starts, tokens, cotangent, qkv_weight, proj_weight, small, scale):
    anyspace = pl.BlockSpec(memory_space=pl.ANY)
    vmem = pl.BlockSpec(memory_space=pltpu.VMEM)
    smem = pl.BlockSpec(memory_space=pltpu.SMEM)
    buffers = tuple(SCRATCH.values()) + tuple(COMM.values())
    return pl.pallas_call(
        functools.partial(kernel, scale),
        out_shape=[
            jax.ShapeDtypeStruct((ROWS, D), BF16),
            jax.ShapeDtypeStruct((32, 3072), F32),
            jax.ShapeDtypeStruct((32, 1024), F32),
            jax.ShapeDtypeStruct((32, 512), F32),
        ],
        in_specs=[smem, smem, vmem, vmem, anyspace, anyspace, anyspace],
        out_specs=[vmem] * 4,
        scratch_shapes=[pltpu.VMEM(*b) for b in buffers]
        + [
            pltpu.SemaphoreType.DMA((5, GATHER_SEMS)),
            pltpu.SemaphoreType.DMA((5, GATHER_SEMS)),
            pltpu.SemaphoreType.DMA((6, REDUCE_SEMS)),
            pltpu.SemaphoreType.DMA((6, REDUCE_SEMS)),
            pltpu.SemaphoreType.DMA((14,)),
        ],
        compiler_params=pltpu.CompilerParams(
            collective_id=0, has_side_effects=True, vmem_limit_bytes=63 * 2**20
        ),
        name="fused",
    )(counts, starts, tokens, cotangent, qkv_weight, proj_weight, small)


def per_device(
    tokens, cotangent, patch_count, image_starts, qkv_weight, proj_weight, norm_gain, norm_shift
):
    small = jnp.pad(jnp.stack([norm_gain, norm_shift], axis=1), ((0, 0), (0, 126)))
    everyone = lax.axis_size("dp") * lax.axis_size("fsdp")
    scale = 1.0 / math.sqrt(tokens.shape[0] * everyone)
    grad_block, qkv_grad, proj_grad, small_grad = fused(
        patch_count, image_starts, tokens, cotangent, qkv_weight, proj_weight, small, scale
    )
    return (grad_block, qkv_grad, proj_grad, small_grad[:, 0], small_grad[:, 1])


def solution(mesh):
    placed = (
        P(("dp", "fsdp"), None),
        P(("dp", "fsdp"), None),
        P(("dp", "fsdp")),
        P(("dp", "fsdp"), None),
        P("fsdp", None),
        P("fsdp", None),
        P("fsdp"),
        P("fsdp"),
    )
    return jax.shard_map(
        per_device,
        mesh=mesh,
        in_specs=placed,
        out_specs=(P(("dp", "fsdp"), None), P("fsdp", None), P("fsdp", None), P("fsdp"), P("fsdp")),
        check_vma=False,
    )
```

time: 428 us -> 136 us (0.32); the launches traced: 420 us -> 136 us
  waiting for transfers between devices: 268 us -> 0 us
  Pallas kernels: 0 us -> 128 us
  matrix products: 70.3 us -> 0 us
  local copies, waits for them, and re-layouts: 26.5 us -> 6.65 us
  blocking collectives: 17.1 us -> 0 us
  between operations: 14.9 us -> 1.31 us
  starting transfers between devices: 11.8 us -> 0 us
  other arithmetic: 11.4 us -> 0.01 us
    reduce_scatter x1 -> x0, waiting for transfers between devices: 158 us -> none  [sent_together(): result = lax.psum_scatter(both, axis, scatter_dimension=dim, tiled=True)]
    pallas_call x0 -> x1, Pallas kernels: none -> 128 us  [fused(): pl.pallas_call(functools.partial(kernel, scale), out_shape=[jax.ShapeDtyp...]
    all_gather x1 -> x0, waiting for transfers between devices: 66.5 us -> none  [side_by_side(): result, at, done = (lax.all_gather(both, axis, axis=dim, tiled=True), 0, [])]
    dot_general x10 -> x0, matrix products: 64.7 us -> none  [the longest x1 15.6 us: block_backward(): jnp.einsum('hqk,khe->qhe', grad_scores, keys, preferred_element_type=jnp....]
    all_to_all x3 -> x0, waiting for transfers between devices: 43.2 us -> none  [copy_for_each(): lax.all_to_all(jnp.broadcast_to(shard[None], (size, *shard.shape)), axis,...]
    all_to_all x1 -> x0, blocking collectives: 17.1 us -> none  [copy_for_each(): lax.all_to_all(jnp.broadcast_to(shard[None], (size, *shard.shape)), axis,...]
    concatenate x2 -> x0, local copies, waits for them, and re-layouts: 14.8 us -> none  [the longest x1 13 us: sent_together(): jnp.concatenate([a.reshape(*a.shape[:along], w) for a, w in zip(arrays, w...]
    all_to_all x3 -> x0, starting transfers between devices: 11.7 us -> none  [copy_for_each(): lax.all_to_all(jnp.broadcast_to(shard[None], (size, *shard.shape)), axis,...]
  transfers between devices with their start and end apart: 5 -> 0, of which waited for: 5 -> 0; matrix products, arithmetic and copies ran while one was open for 3% -> 0% of each run, Pallas kernels for 0% -> 0%
where the time goes in v2:
time: 136 us
  Pallas kernels  128 us (94%)
  local copies, waits for them, and re-layouts  6.65 us (5%)
    pallas_call x1, Pallas kernels, fused(): pl.pallas_call(functools.partial(kernel, scale), out_shape=[jax.ShapeDtyp...  128 us
    unnamed x11, local copies, waits for them, and re-layouts  4.45 us

profile of v2, /device:TPU:32, one launch (start us, length us, event | category | flops | bytes accessed | tf_op | source)
XLA Modules:
  0.0 135.9 jit_solution(3956435892942324415)
XLA Ops:
  0.6 0.0 copy-start.2
  0.6 0.0 copy-start.3
  0.7 0.6 copy-done.2
  1.3 0.0 copy-done.3
  1.3 0.1 copy.17
  1.4 0.6 pad.4.small_ref
  2.7 127.9 %fused.1 = (bf16[384,1024]{1,0:T(8,128)(2,1)}, f32[32,3072]{1,0:T(8,128)}, f32[32,1024]{1,0:T(8,128)}, f32[32,512]{1,0:T(8,128)}) custom-call(s32[1]{0:T(128)S(6)} %copy.21.count_ref, s32[1,8]{1,0:T(1,128)} %starts_ref.1, bf16[384,1024]{1,0:T(8,128)(2,1)} %tok_ref.1, bf16[384,1024]{1,0:T(8,128)(2,1)} %cot_ref.1, bf16[32,3072]{1,0:T(8,128)(2,1)} %qkv_ref.1, ...), custom_call_target="tpu_custom_call" | custom-call | tf_op jit(solution)/shard_map/fused/pallas_call | solution.py:643
  130.6 1.5 %slice_reduce_fusion = (f32[32]{0:T(128)}, f32[32]{0:T(128)}) fusion(f32[32,512]{1,0:T(8,128)} %get-tuple-element.12), kind=kLoop, calls=%fused_computation | loop fusion | bytes 512 | tf_op jit(solution)/shard_map/slice | solution.py:677
  132.1 0.0 copy-start
  132.1 2.1 %copy.22 = bf16[384,1024]{1,0:T(8,128)(2,1)} copy(bf16[384,1024]{1,0:T(8,128)(2,1)} %get-tuple-element.20) | data formatting | bytes 1572864
  134.2 0.0 copy-done
  134.2 0.0 copy-start.1
  134.2 0.7 copy.23
  135.0 0.3 copy-done.1
  135.2 0.7 copy.24
  (1 shorter events, 0.0 us)
Async XLA Ops:
  0.6 0.7 copy-start.2
  0.6 0.7 copy-start.3
  132.1 2.1 %copy-start = (f32[32,3072]{1,0:T(8,128)S(1)}, f32[32,3072]{1,0:T(8,128)}, u32[]{:S(2)}) copy-start(f32[32,3072]{1,0:T(8,128)} %get-tuple-element.21) | copy-start | bytes 1179652
  134.2 1.0 copy-start.1

commit v3 on v2

v3 whole, which is shorter than its diff:
```python
import functools
import math

import jax
import jax.numpy as jnp
from jax import lax
from jax.experimental import pallas as pl
from jax.experimental.pallas import tpu as pltpu
from jax.sharding import PartitionSpec as P

MESH = pl.DeviceIdType.MESH
F32 = jnp.float32
BF16 = jnp.bfloat16
D = 1024
ROWS = 384


def nn(a, b):
    return lax.dot_general(a, b, (((1,), (0,)), ((), ())), preferred_element_type=F32)


def nt(a, b):
    return lax.dot_general(a, b, (((1,), (1,)), ((), ())), preferred_element_type=F32)


def tn(a, b):
    return lax.dot_general(a, b, (((0,), (0,)), ((), ())), preferred_element_type=F32)


class Place:
    def __init__(self):
        dp, fsdp = lax.axis_index("dp"), lax.axis_index("fsdp")
        self.y, self.zhi = dp // 2, dp % 2
        self.c = fsdp % 2
        chip = fsdp // 2
        self.x, self.zlo = chip // 4, chip % 4
        self.z = self.zhi * 4 + self.zlo

    def at(self, dx=0, dy=0, dz=0, flip=0):
        x = (self.x + dx + 4) % 4
        y = (self.y + dy + 4) % 4
        z = (self.z + dz + 8) % 8
        c = self.c + flip * (1 - 2 * self.c)
        return {"dp": y * 2 + z // 4, "fsdp": (x * 4 + z % 4) * 2 + c}

    def along_x(self, d):
        return self.at(dx=(1 - self.c) * d, dz=self.c * d)

    def along_z(self, d):
        return self.at(dx=self.c * d, dz=(1 - self.c) * d)

    def chip(self, i, j):
        x = (self.x + (1 - self.c) * i + self.c * j + 8) % 4
        z = (self.zlo + self.c * i + (1 - self.c) * j + 8) % 4
        return x, z

    def sibling(self):
        return self.at(flip=1)

    def first(self, d):
        return self.at(dx=self.c * d, dy=(1 - self.c) * d)

    def second(self, d):
        return self.at(dx=(1 - self.c) * d, dy=self.c * d)

    def quarter(self, d1, d2):
        x = (self.x + self.c * d1 + (1 - self.c) * d2) % 4
        y = (self.y + (1 - self.c) * d1 + self.c * d2) % 4
        return x, y

    def all(self):
        return (
            [self.sibling()]
            + [self.at(dx=d) for d in (1, 2, 3)]
            + [self.at(dy=d) for d in (1, 2, 3)]
            + [self.at(dz=d) for d in range(1, 8)]
        )


def enter(devices, meanwhile):
    barrier = pltpu.get_barrier_semaphore()
    for device in devices:
        pl.semaphore_signal(barrier, inc=1, device_id=device, device_id_type=MESH)
    meanwhile()
    pl.semaphore_wait(barrier, len(devices))


class Copies:
    def __init__(self, place, send_sems, recv_sems):
        self.place, self.send_sems, self.recv_sems = place, send_sems, recv_sems

    def copy(self, src, dst, n, device):
        return pltpu.make_async_remote_copy(
            src_ref=src,
            dst_ref=dst,
            send_sem=self.send_sems.at[n],
            recv_sem=self.recv_sems.at[n],
            device_id=device,
            device_id_type=MESH,
        )

    def start(self, src, dst, n, device):
        self.copy(src, dst, n, device).start()

    def arrived(self, ref, n):
        self.copy(ref, ref, n, self.place.sibling()).wait_recv()

    def left(self, ref, n):
        self.copy(ref, ref, n, self.place.sibling()).wait_send()


GATHER_SEMS = 36
ORDER = (0, -1, 1, 2)


class Gather(Copies):
    def __init__(self, place, buffer, send_sems, recv_sems):
        super().__init__(place, send_sems, recv_sems)
        self.buffer = buffer

    def block(self, i, j, half=None):
        x, z = self.place.chip(i, j)
        ref = self.buffer.at[x, z, self.place.c]
        return ref if half is None else ref.at[pl.ds(half * 16, 16)]

    def forward(self, ref, n, device):
        self.start(ref, ref, n, device)

    def to_second(self, i):
        self.forward(self.block(i, 0), 4 + 4 * (i % 4), self.place.along_z(1))
        self.forward(self.block(i, 0), 5 + 4 * (i % 4), self.place.along_z(-1))
        self.to_sibling(i, 0)

    def to_sibling(self, i, j):
        self.forward(self.block(i, j), 20 + 4 * (i % 4) + (j % 4), self.place.sibling())

    def stage0(self):
        self.forward(self.block(0, 0), 0, self.place.along_x(1))
        self.forward(self.block(0, 0), 1, self.place.along_x(-1))
        self.to_second(0)

    def stage1(self):
        self.arrived(self.block(-1, 0), 0)
        self.forward(self.block(-1, 0, 0), 2, self.place.along_x(1))
        self.arrived(self.block(1, 0), 1)
        self.forward(self.block(1, 0, 1), 3, self.place.along_x(-1))
        self.to_second(-1)
        self.to_second(1)

    def stage2(self):
        self.arrived(self.block(2, 0, 0), 2)
        self.arrived(self.block(2, 0, 1), 3)
        self.to_second(2)

    def stage3(self):
        for i in ORDER:
            k = i % 4
            self.arrived(self.block(i, -1), 4 + 4 * k)
            self.forward(self.block(i, -1, 0), 6 + 4 * k, self.place.along_z(1))
            self.to_sibling(i, -1)
            self.arrived(self.block(i, 1), 5 + 4 * k)
            self.forward(self.block(i, 1, 1), 7 + 4 * k, self.place.along_z(-1))
            self.to_sibling(i, 1)

    def stage4(self):
        for i in ORDER:
            k = i % 4
            self.arrived(self.block(i, 2, 0), 6 + 4 * k)
            self.arrived(self.block(i, 2, 1), 7 + 4 * k)
            self.to_sibling(i, 2)

    def stage5(self):
        for i in range(4):
            for j in range(4):
                x, z = self.place.chip(j, i)
                self.arrived(self.buffer.at[x, z, 1 - self.place.c], 20 + 4 * i + j)

    def drain(self):
        whole, half = self.block(0, 0), self.block(0, 0, 0)
        for n in range(GATHER_SEMS):
            self.left(half if n in (2, 3) or (n < 20 and n % 4 > 1) else whole, n)


REDUCE_SEMS = 21


def reduce_shapes(half):
    return dict(
        R=(4, 4, 4, 16, half),
        A=(4, 4, 4, 16, half),
        T=(2, 2, 4, 16, half),
        U=(2, 4, 4, 16, half),
        B=(4, 4, 16, half),
        Y=(3, 4, 16, half),
        C=(4, 16, half),
        V=(8, 16, half),
        E=(16, half),
        O=(4, 16, half),
    )


REDUCE_NAMES = tuple(reduce_shapes(128))


class Reduce(Copies):
    def __init__(self, place, term, buffers, send_sems, recv_sems):
        super().__init__(place, send_sems, recv_sems)
        self.term = term
        for name, ref in zip(REDUCE_NAMES, buffers):
            setattr(self, name, ref)

    def stage0(self):
        at = self.place

        @pl.when(at.c == 1)
        def _():
            for d1 in (2, 1, 3, 0):
                src = self.term.at[:, :, 0, (at.y + d1) % 4]
                self.start(src, self.R.at[d1], d1, at.sibling())

        @pl.when(at.c == 0)
        def _():
            for d1 in (2, 1, 3, 0):
                src = self.term.at[(at.x + d1) % 4, :, 1]
                self.start(src, self.R.at[d1], d1, at.sibling())

    def pair(self, d1):
        at = self.place
        self.arrived(self.R.at[d1], d1)
        for d2 in range(4):
            x, y = at.quarter(d1, d2)
            for z in range(4):
                m = (1 - at.c) * x + at.c * z
                n = (1 - at.c) * z + at.c * y
                both = self.term[x, z, at.c, y].astype(F32) + self.R[d1, m, n].astype(F32)
                self.A[d1, d2, z] = both.astype(BF16)

    def stage1(self):
        at = self.place
        self.pair(2)
        self.start(self.A.at[2, pl.ds(0, 2)], self.T.at[0], 4, at.first(1))
        self.start(self.A.at[2, pl.ds(2, 2)], self.T.at[1], 5, at.first(-1))
        self.pair(1)
        self.pair(3)
        self.pair(0)

    def stage2(self):
        at = self.place
        self.arrived(self.T.at[0], 4)
        self.A[1, 0:2] = (self.A[1, 0:2].astype(F32) + self.T[0].astype(F32)).astype(BF16)
        self.start(self.A.at[1], self.U.at[0], 6, at.first(1))
        self.arrived(self.T.at[1], 5)
        self.A[3, 2:4] = (self.A[3, 2:4].astype(F32) + self.T[1].astype(F32)).astype(BF16)
        self.start(self.A.at[3], self.U.at[1], 7, at.first(-1))

    def stage3(self):
        at = self.place
        self.arrived(self.U.at[0], 6)
        self.arrived(self.U.at[1], 7)
        for d2 in (2, 1, 3, 0):
            total = self.A[0, d2].astype(F32) + self.U[0, d2].astype(F32)
            self.B[d2] = (total + self.U[1, d2].astype(F32)).astype(BF16)
            if d2:
                self.start(self.B.at[d2], self.Y.at[d2 - 1], 7 + d2, at.second(d2))

    def stage4(self):
        at = self.place
        for d2 in (1, 3, 2):
            self.arrived(self.Y.at[d2 - 1], 7 + d2)
        total = self.B[0].astype(F32) + self.Y[0].astype(F32)
        total = total + self.Y[1].astype(F32) + self.Y[2].astype(F32)
        self.C[...] = total.astype(BF16)
        for d in (4, 3, 5, 2, 6, 1, 7):
            self.start(self.C.at[(at.zlo + d) % 4], self.V.at[at.z], 10 + d, at.at(dz=d))
        self.V[at.z] = self.C[at.zlo]

    def stage5(self):
        at = self.place
        for d in (1, 7, 2, 6, 3, 5, 4):
            self.arrived(self.V.at[(at.z + 8 - d) % 8], 10 + d)
        total = self.V[0].astype(F32)
        for z in range(1, 8):
            total = total + self.V[z].astype(F32)
        self.E[...] = total.astype(BF16)
        for d in (2, 1, 3):
            self.start(self.E, self.O.at[at.y], 17 + d, at.at(dy=d))

    def stage6(self, write):
        at = self.place
        for d in (1, 3, 2):
            self.arrived(self.O.at[(at.y - d + 4) % 4], 17 + d)
        self.O[at.y] = self.E[...]
        for r in range(2):
            for k in range(2):
                write(r, k, self.O[2 * r + k])

    def drain(self):
        for d1 in range(4):
            self.left(self.R.at[d1], d1)
        self.left(self.T.at[0], 4)
        self.left(self.T.at[1], 5)
        self.left(self.U.at[0], 6)
        self.left(self.U.at[1], 7)
        for d2 in (1, 2, 3):
            self.left(self.B.at[0], 7 + d2)
        for n in range(11, 21):
            self.left(self.E, n)


SMALL_SEMS = 14


class Small(Copies):
    def __init__(self, place, tile, slots, send_sems, recv_sems):
        super().__init__(place, send_sems, recv_sems)
        self.tile, self.slots = tile, slots

    def step(self, n):
        at = self.place
        size, mine, first = ((4, at.x, 0), (4, at.y, 3), (8, at.z, 6), (2, at.c, 13))[n]
        other = (
            lambda d: at.at(dx=d),
            lambda d: at.at(dy=d),
            lambda d: at.at(dz=d),
            lambda d: at.sibling(),
        )[n]
        return size, mine, first, other

    def send(self, n):
        size, mine, first, other = self.step(n)
        for d in range(1, size):
            self.start(self.tile.at[n], self.slots.at[n, mine], first + d - 1, other(d))

    def receive(self, n):
        size, mine, first, _ = self.step(n)
        for d in range(1, size):
            self.arrived(self.slots.at[n, (mine - d + size) % size], first + d - 1)
        self.slots[n, mine] = self.tile[n]
        total = self.slots[n, 0].astype(F32)
        for k in range(1, size):
            total = total + self.slots[n, k].astype(F32)
        return total

    def stage0(self):
        self.send(0)

    def stage1(self):
        self.tile[1] = self.receive(0).astype(BF16)
        self.send(1)

    def stage2(self):
        self.tile[2] = self.receive(1).astype(BF16)
        self.send(2)

    def stage3(self):
        self.tile[3] = self.receive(2).astype(BF16)
        self.send(3)

    def stage4(self, write):
        write(self.receive(3))

    def drain(self):
        for n in range(SMALL_SEMS):
            self.left(self.tile.at[0], n)


class Timeline:
    def __init__(self):
        self.now, self.live = 0.0, []

    def add(self, stages):
        work = [self.now, len(self.live), list(stages)]
        self.live.append(work)
        self.run(self.now)
        return work

    def step(self, work):
        call, latency = work[2].pop(0)
        call()
        work[0] = max(self.now, work[0]) + latency

    def run(self, until):
        while True:
            ready = [w for w in self.live if w[2] and w[0] <= until]
            if not ready:
                return
            self.step(min(ready, key=lambda w: (w[0], w[1])))

    def spend(self, time):
        self.now += time
        self.run(self.now)

    def finish(self, work):
        while work[2]:
            self.now = max(self.now, min(w[0] for w in self.live if w[2]))
            self.run(self.now)


SCRATCH = {
    "normed": ((384, 1024), F32),
    "inverse": ((384, 128), F32),
    "hidden": ((384, 1024), BF16),
    "hidden_t": ((1024, 384), BF16),
    "mcot": ((384, 1024), BF16),
    "live": ((384, 128), F32),
    "ga": ((4, 384, 256), BF16),
    "att": ((4, 384, 256), BF16),
    "qkv": ((2, 384, 768), BF16),
    "dqkv": ((384, 768), BF16),
    "bias": ((384, 384), F32),
    "gains": ((2, 1024), F32),
    "probs": ((2, 4, 384, 384), F32),
    "low": ((2, 384, 384), BF16),
    "dscores": ((2, 384, 384), BF16),
    "gh": ((384, 1024), F32),
    "own": ((128, 128), F32),
    "own_low": ((32, 128), BF16),
    "sums": ((16, 128), F32),
}


def own_small(S, gain_ref, shift_ref):
    S["own"][...] = jnp.zeros((128, 128), F32)
    S["own"][0:1, 0:32] = gain_ref[...].astype(F32)
    S["own"][1:2, 0:32] = shift_ref[...].astype(F32)
    S["own_low"][...] = S["own"][...].T[0:32].astype(BF16)


def prologue_tokens(S, tok_ref, cot_ref, count_ref, starts_ref):
    source = tok_ref[...].astype(F32)
    center = jnp.mean(source, axis=1, keepdims=True)
    centered = source - center
    variance = jnp.mean(centered * centered, axis=1, keepdims=True)
    inverse = lax.rsqrt(variance + 1e-06)
    S["normed"][...] = centered * inverse
    S["inverse"][...] = jnp.broadcast_to(inverse, (ROWS, 128))
    count = count_ref[0]
    down = lax.broadcasted_iota(jnp.int32, (ROWS, 1), 0)
    across = lax.broadcasted_iota(jnp.int32, (1, ROWS), 1)
    seg_down = jnp.zeros((ROWS, 1), jnp.int32)
    seg_across = jnp.zeros((1, ROWS), jnp.int32)
    for j in range(8):
        start = starts_ref[0, j]
        seg_down = seg_down + jnp.where(down >= start, 1, 0)
        seg_across = seg_across + jnp.where(across >= start, 1, 0)
    seg_down = jnp.where(down < count, seg_down, -1)
    seg_across = jnp.where(across < count, seg_across, -2)
    S["bias"][...] = jnp.where(seg_down == seg_across, 0.0, -1e30).astype(F32)
    alive = lax.broadcasted_iota(jnp.int32, (ROWS, 128), 0) < count
    S["live"][...] = jnp.where(alive, 1.0, 0.0).astype(F32)
    alive = S["live"][:, 0:1] > 0.5
    S["mcot"][...] = jnp.where(alive, cot_ref[...].astype(F32), 0.0).astype(BF16)


def prologue_hidden(S):
    small = S["Wps"][:, :, :, :, 1024:1152].reshape(1024, 128).astype(F32)
    S["gains"][...] = small.T[0:2, :]
    gain = S["gains"][0:1, :]
    shift = S["gains"][1:2, :]
    S["hidden"][...] = (S["normed"][...] * gain + shift).astype(BF16)
    S["hidden_t"][...] = S["hidden"][...].T


def grads_attended(S):
    for g in range(4):
        part = S["Wps"][g, :, :, :, 0:1024].reshape(256, 1024)
        S["ga"][g] = nt(S["mcot"][...], part).astype(BF16)


def own(a, h):
    first = lax.broadcasted_iota(jnp.int32, (ROWS, 128), 1) < 64
    zero = jnp.zeros_like(a)
    return jnp.where(first, a, zero) if h == 0 else jnp.where(first, zero, a)


def lanes(ref, pair, part):
    return ref[:, part * 256 + pair * 128 : part * 256 + pair * 128 + 128]


def forward(S, g, spend):
    qkv, slot = S["qkv"].at[g % 2], g % 2
    for n in range(3):
        weight = S["Wg"][g, :, :, :, :, n * 256 : n * 256 + 256].reshape(1024, 256)
        part = nn(S["hidden"][...], weight).astype(BF16)
        qkv[:, n * 256 : n * 256 + 256] = part * jnp.asarray(0.125, BF16) if n == 0 else part
    spend(0.9)
    for pair in range(2):
        q2, k2, v2 = (lanes(qkv, pair, n) for n in range(3))
        for h in range(2):
            scores = nt(own(q2, h), k2) + S["bias"][...]
            row_max = jnp.max(scores, axis=1, keepdims=True)
            expon = jnp.exp(scores - row_max)
            probs = expon * (1.0 / jnp.sum(expon, axis=1, keepdims=True))
            S["probs"][slot, 2 * pair + h] = probs
            S["low"][h] = probs.astype(BF16)
        att = sum(nn(S["low"][h], own(v2, h)) for h in range(2))
        S["att"][g, :, pair * 128 : pair * 128 + 128] = att.astype(BF16)
        spend(1.0)


def backward(S, g, spend):
    qkv, slot = S["qkv"].at[g % 2], g % 2
    for pair in range(2):
        q2, k2, v2 = (lanes(qkv, pair, n) for n in range(3))
        o2 = S["ga"][g, :, pair * 128 : pair * 128 + 128]
        for h in range(2):
            probs = S["probs"][slot, 2 * pair + h]
            grad_probs = nt(own(o2, h), v2)
            delta = jnp.sum(probs * grad_probs, axis=1, keepdims=True)
            S["dscores"][h] = (probs * (grad_probs - delta)).astype(BF16)
            S["low"][h] = probs.astype(BF16)
        spend(0.8)
        dv = sum(tn(S["low"][h], own(o2, h)) for h in range(2))
        dq = sum(nn(S["dscores"][h], own(k2, h)) for h in range(2)) * 0.125
        dk = sum(tn(S["dscores"][h], own(q2, h)) for h in range(2))
        for n, part in enumerate((dq, dk, dv)):
            start = n * 256 + pair * 128
            S["dqkv"][:, start : start + 128] = part.astype(BF16)
        spend(0.8)


def weight_grads(S, g):
    for m in range(4):
        part = nn(S["hidden_t"][m * 256 : m * 256 + 256], S["dqkv"][...]).astype(BF16)
        part = part.reshape(4, 2, 2, 16, 768)
        for r in range(2):
            for k in range(2):
                S["G"][g, m, :, :, 2 * r + k] = part[:, :, r, :, k * 384 : k * 384 + 384]


def hidden_grads(S, g):
    for n in range(4):
        part = nt(S["dqkv"][...], S["Wg"][g, n].reshape(256, 768))
        columns = slice(n * 256, n * 256 + 256)
        S["gh"][:, columns] = part if g == 0 else S["gh"][:, columns] + part


def proj_grads(S):
    for g in range(4):
        part = tn(S["att"][g], S["mcot"][...]).astype(BF16).reshape(4, 2, 2, 16, 1024)
        for r in range(2):
            for k in range(2):
                S["Gp"][g, :, :, 2 * r + k] = part[:, :, r, :, k * 512 : k * 512 + 512]


def small_grads(S):
    gh = S["gh"][...]
    gain_term = jnp.sum(gh * S["normed"][...], axis=0, keepdims=True)
    shift_term = jnp.sum(gh, axis=0, keepdims=True)
    for r in range(8):
        S["sums"][r : r + 1, :] = gain_term[:, r * 128 : r * 128 + 128]
        S["sums"][8 + r : 9 + r, :] = shift_term[:, r * 128 : r * 128 + 128]
    S["tile"][0] = S["sums"][...].astype(BF16)


def token_grads(S):
    normed = S["normed"][...]
    grad_normed = S["gh"][...] * S["gains"][0:1, :]
    inner = grad_normed - jnp.mean(grad_normed, axis=1, keepdims=True)
    inner = inner - normed * jnp.mean(grad_normed * normed, axis=1, keepdims=True)
    S["gh"][...] = S["inverse"][:, 0:1] * inner


COMM = {}
for _name, _shape in reduce_shapes(384).items():
    COMM["g_" + _name] = ((4,) + _shape, BF16)
for _name, _shape in reduce_shapes(512).items():
    COMM["p_" + _name] = (_shape, BF16)
COMM["Wg"] = ((4, 4, 4, 2, 32, 768), BF16)
COMM["Wps"] = ((4, 4, 2, 32, 1152), BF16)
COMM["G"] = ((4, 4, 4, 2, 4, 16, 384), BF16)
COMM["Gp"] = ((4, 4, 2, 4, 16, 512), BF16)
COMM["tile"] = ((4, 16, 128), BF16)
COMM["slots"] = ((4, 8, 16, 128), BF16)


def kernel(
    count_ref,
    starts_ref,
    tok_ref,
    cot_ref,
    qkv_ref,
    proj_ref,
    gain_ref,
    shift_ref,
    out_ref,
    qkv_out,
    proj_out,
    gain_out,
    shift_out,
    *scratch,
):
    S = dict(zip(tuple(SCRATCH) + tuple(COMM), scratch))
    gs, gr, rs, rr, ss, sr, ls = scratch[len(S) :]
    place = Place()
    x, z, c = place.x, place.zlo, place.c
    time = Timeline()

    own_small(S, gain_ref, shift_ref)
    local = []
    for n, (src, dst) in enumerate(
        [
            (proj_ref, S["Wps"].at[x, z, c, :, pl.ds(0, 1024)]),
            (S["own_low"], S["Wps"].at[x, z, c, :, pl.ds(1024, 128)]),
        ]
        + [
            (
                qkv_ref.at[:, pl.ds(part * 1024 + g * 256, 256)],
                S["Wg"].at[g, x, z, c, :, pl.ds(part * 256, 256)],
            )
            for g in range(4)
            for part in range(3)
        ]
    ):
        copy = pltpu.make_async_copy(src, dst, ls.at[n])
        copy.start()
        local.append(copy)

    enter(place.all(), lambda: prologue_tokens(S, tok_ref, cot_ref, count_ref, starts_ref))
    for copy in local:
        copy.wait()

    buffers = [S["Wps"]] + [S["Wg"].at[g] for g in range(4)]
    gathers = [Gather(place, b, gs.at[k], gr.at[k]) for k, b in enumerate(buffers)]

    def gather(k):
        piece = gathers[k]
        calls = (piece.stage0, piece.stage1, piece.stage2, piece.stage3, piece.stage4, piece.stage5)
        return time.add(zip(calls, GATHER_TIMES))

    def write_group(g):
        def write(r, k, value):
            rows = slice(r * 16, r * 16 + 16)
            if k == 0:
                qkv_out[rows, g * 256 : g * 256 + 256] = value[:, 0:256]
                qkv_out[rows, 1024 + g * 256 : 1152 + g * 256] = value[:, 256:384]
            else:
                qkv_out[rows, 1152 + g * 256 : 1280 + g * 256] = value[:, 0:128]
                qkv_out[rows, 2048 + g * 256 : 2304 + g * 256] = value[:, 128:384]

        return write

    def write_proj(r, k, value):
        proj_out[r * 16 : r * 16 + 16, k * 512 : k * 512 + 512] = value

    def write_small(total):
        S["sums"][...] = total
        place_in_row = place.zlo * 2 + place.c
        for first, out in ((0, gain_out), (8, shift_out)):
            row = S["sums"][pl.ds(first + place.x * 2 + place.zlo // 2, 1), :]
            value = jnp.zeros((1, 32), F32)
            for k in range(4):
                value = jnp.where(place_in_row % 4 == k, row[:, k * 32 : k * 32 + 32], value)
            out[...] = value

    reduces = []

    def reduce(term, names, sem, write):
        piece = Reduce(place, term, names, rs.at[sem], rr.at[sem])
        reduces.append(piece)
        calls = (piece.stage0, piece.stage1, piece.stage2, piece.stage3, piece.stage4)
        calls += (piece.stage5, functools.partial(piece.stage6, write))
        return time.add(zip(calls, REDUCE_TIMES))

    works = []
    for k in GATHER_ORDER:
        works.append((k, gather(k)))
        time.now += GATHER_GAP
    works = [w for _, w in sorted(works, key=lambda pair: pair[0])]
    time.now = 0.0
    time.finish(works[0])
    prologue_hidden(S)
    time.spend(1.0)
    time.finish(works[1])
    forward(S, 0, time.spend)
    grads_attended(S)
    time.spend(1.0)
    for g in range(4):
        if g < 3:
            time.finish(works[g + 2])
            forward(S, g + 1, time.spend)
            if g == 2:
                proj_grads(S)
                reduce(S["Gp"], [S["p_" + n] for n in REDUCE_NAMES], 4, write_proj)
        backward(S, g, time.spend)
        weight_grads(S, g)
        names = [S["g_" + n].at[g] for n in REDUCE_NAMES]
        reduce(S["G"].at[g], names, g, write_group(g))
        time.spend(0.8)
        hidden_grads(S, g)
        time.spend(1.0)
    small_grads(S)
    small = Small(place, S["tile"], S["slots"], ss, sr)
    calls = (small.stage0, small.stage1, small.stage2, small.stage3)
    calls += (functools.partial(small.stage4, write_small),)
    time.add(zip(calls, SMALL_TIMES))
    token_grads(S)
    out = pltpu.make_async_copy(S["gh"], out_ref, ls.at[0])
    out.start()
    time.spend(0.8)
    for work in list(time.live):
        time.finish(work)
    out.wait()
    for piece in gathers + reduces + [small]:
        piece.drain()


GATHER_ORDER = (0, 1, 2, 3, 4)
GATHER_GAP = 3.0
GATHER_TIMES = (3.0, 3.0, 3.0, 4.0, 2.5, 0.0)
REDUCE_TIMES = (2.5, 3.0, 4.0, 3.5, 4.0, 3.0, 0.0)
SMALL_TIMES = (2.5, 2.5, 4.0, 1.5, 0.0)


def fused(counts, starts, tokens, cotangent, qkv_weight, proj_weight, gain, shift):
    anyspace = pl.BlockSpec(memory_space=pl.ANY)
    vmem = pl.BlockSpec(memory_space=pltpu.VMEM)
    smem = pl.BlockSpec(memory_space=pltpu.SMEM)
    buffers = tuple(SCRATCH.values()) + tuple(COMM.values())
    return pl.pallas_call(
        kernel,
        out_shape=[
            jax.ShapeDtypeStruct((ROWS, D), F32),
            jax.ShapeDtypeStruct((32, 3072), BF16),
            jax.ShapeDtypeStruct((32, 1024), BF16),
            jax.ShapeDtypeStruct((1, 32), F32),
            jax.ShapeDtypeStruct((1, 32), F32),
        ],
        in_specs=[smem, smem, vmem, vmem, anyspace, anyspace, vmem, vmem],
        out_specs=[anyspace] + [vmem] * 4,
        scratch_shapes=[pltpu.VMEM(*b) for b in buffers]
        + [
            pltpu.SemaphoreType.DMA((5, GATHER_SEMS)),
            pltpu.SemaphoreType.DMA((5, GATHER_SEMS)),
            pltpu.SemaphoreType.DMA((5, REDUCE_SEMS)),
            pltpu.SemaphoreType.DMA((5, REDUCE_SEMS)),
            pltpu.SemaphoreType.DMA((SMALL_SEMS,)),
            pltpu.SemaphoreType.DMA((SMALL_SEMS,)),
            pltpu.SemaphoreType.DMA((14,)),
        ],
        compiler_params=pltpu.CompilerParams(
            collective_id=0, has_side_effects=True, vmem_limit_bytes=67043328
        ),
        name="fused",
    )(counts, starts, tokens, cotangent, qkv_weight, proj_weight, gain, shift)


def per_device(
    tokens, cotangent, patch_count, image_starts, qkv_weight, proj_weight, norm_gain, norm_shift
):
    everyone = lax.axis_size("dp") * lax.axis_size("fsdp")
    scale = 1.0 / math.sqrt(tokens.shape[0] * everyone)
    through_norm, qkv_grad, proj_grad, gain_grad, shift_grad = fused(
        patch_count,
        image_starts,
        tokens,
        cotangent,
        qkv_weight,
        proj_weight,
        norm_gain.reshape(1, -1),
        norm_shift.reshape(1, -1),
    )
    return (
        (cotangent.astype(F32) + through_norm).astype(BF16),
        qkv_grad.astype(F32) * scale,
        proj_grad.astype(F32) * scale,
        gain_grad.reshape(-1) * scale,
        shift_grad.reshape(-1) * scale,
    )


def solution(mesh):
    placed = (
        P(("dp", "fsdp"), None),
        P(("dp", "fsdp"), None),
        P(("dp", "fsdp")),
        P(("dp", "fsdp"), None),
        P("fsdp", None),
        P("fsdp", None),
        P("fsdp"),
        P("fsdp"),
    )
    return jax.shard_map(
        per_device,
        mesh=mesh,
        in_specs=placed,
        out_specs=(P(("dp", "fsdp"), None), P("fsdp", None), P("fsdp", None), P("fsdp"), P("fsdp")),
        check_vma=False,
    )
```

time: 136 us -> 115 us (0.85)
  Pallas kernels: 128 us -> 108 us
  local copies, waits for them, and re-layouts: 6.65 us -> 0.02 us
  other arithmetic: 0.01 us -> 4.75 us
    pallas_call x1, Pallas kernels: 128 us -> 108 us  [fused(): pl.pallas_call(kernel, out_shape=[jax.ShapeDtypeStruct((ROWS, D), F32), j...]
    unnamed x11 -> x8, local copies, waits for them, and re-layouts: 4.45 us -> 0.02 us
    convert_element_type x0 -> x1, other arithmetic: none -> 2.78 us  [per_device(): (cotangent.astype(F32) + through_norm).astype(BF16)]
    mul x0 -> x3, other arithmetic: none -> 1.96 us  [the longest x1 0.78 us: per_device(): qkv_grad.astype(F32) * scale]
    slice x1 -> x0, local copies, waits for them, and re-layouts: 1.49 us -> none  [per_device(): return (grad_block, qkv_grad, proj_grad, small_grad[:, 0], small_grad[:, 1])]
where the time goes in v3:
time: 115 us; the launch traced here: 114 us
  Pallas kernels  108 us (94%)
  other arithmetic  4.75 us (4%)
  between operations  1.32 us (1%)
    pallas_call x1, Pallas kernels, fused(): pl.pallas_call(kernel, out_shape=[jax.ShapeDtypeStruct((ROWS, D), F32), j...  108 us
    convert_element_type x1, other arithmetic, per_device(): (cotangent.astype(F32) + through_norm).astype(BF16)  2.78 us

profile of v3, /device:TPU:32, one launch (start us, length us, event | category | flops | bytes accessed | tf_op | source)
XLA Modules:
  0.0 114.4 jit_solution(1858828822992626962)
XLA Ops:
  1.3 108.3 %fused.1 = (f32[384,1024]{1,0:T(8,128)}, bf16[32,3072]{1,0:T(8,128)(2,1)}, bf16[32,1024]{1,0:T(8,128)(2,1)}, f32[1,32]{1,0:T(1,128)}, f32[1,32]{1,0:T(1,128)}) custom-call(s32[1]{0:T(128)S(6)} %copy.13.count_ref, s32[1,8]{1,0:T(1,128)} %starts_ref.1, bf16[384,1024]{1,0:T(8,128)(2,1)} %tok_ref.1, bf16[384,1024]{1,0:T(8,128)(2,1)} %cot_ref.1, ...), custom_call_target="tpu_custom_call" | custom-call | tf_op jit(solution)/shard_map/fused/pallas_call | solution.py:720
  109.6 0.0 copy-start.2
  109.6 0.0 copy-start.3
  109.6 0.0 copy-start.1
  109.7 0.0 copy-start
  109.7 2.8 %add_convert_fusion = bf16[384,1024]{1,0:T(8,128)(2,1)} fusion(f32[384,1024]{1,0:T(8,128)} %get-tuple-element.10, bf16[384,1024]{1,0:T(8,128)(2,1)} %cot_ref.1), kind=kLoop, calls=%fused_computation | loop fusion | flops 1179648 | bytes 3145728 | tf_op jit(solution)/shard_map/convert_element_type | solution.py:764
  112.4 0.0 copy-done.2
  112.4 0.0 copy-done.3
  112.4 0.5 multiply_bitcast_fusion
  113.0 0.0 copy-done.1
  113.0 0.7 convert_multiply_fusion.1
  113.6 0.0 copy-done
  113.6 0.8 convert_multiply_fusion
Async XLA Ops:
  109.6 2.8 %copy-start.2 = (f32[1,32]{1,0:T(1,128)S(1)}, f32[1,32]{1,0:T(1,128)}, u32[]{:S(2)}) copy-start(f32[1,32]{1,0:T(1,128)} %get-tuple-element.13) | copy-start | bytes 388
  109.6 2.8 %copy-start.3 = (f32[1,32]{1,0:T(1,128)S(1)}, f32[1,32]{1,0:T(1,128)}, u32[]{:S(2)}) copy-start(f32[1,32]{1,0:T(1,128)} %get-tuple-element.14) | copy-start | bytes 388
  109.6 3.3 %copy-start.1 = (bf16[32,1024]{1,0:T(8,128)(2,1)S(1)}, bf16[32,1024]{1,0:T(8,128)(2,1)}, u32[]{:S(2)}) copy-start(bf16[32,1024]{1,0:T(8,128)(2,1)} %get-tuple-element.12) | copy-start | bytes 196612
  109.7 4.0 %copy-start = (bf16[32,3072]{1,0:T(8,128)(2,1)S(1)}, bf16[32,3072]{1,0:T(8,128)(2,1)}, u32[]{:S(2)}) copy-start(bf16[32,3072]{1,0:T(8,128)(2,1)} %get-tuple-element.11) | copy-start | bytes 589828

commit v4 on v3

--- a/solution.py
+++ b/solution.py
@@ -89,99 +89,99 @@
     def __init__(self, place, send_sems, recv_sems):
         self.place, self.send_sems, self.recv_sems = place, send_sems, recv_sems
 
-    def copy(self, src, dst, n, device):
+    def copy(self, src, dst, out, into, device):
         return pltpu.make_async_remote_copy(
             src_ref=src,
             dst_ref=dst,
-            send_sem=self.send_sems.at[n],
-            recv_sem=self.recv_sems.at[n],
+            send_sem=self.send_sems.at[out],
+            recv_sem=self.recv_sems.at[into],
             device_id=device,
             device_id_type=MESH,
         )
 
-    def start(self, src, dst, n, device):
-        self.copy(src, dst, n, device).start()
-
-    def arrived(self, ref, n):
-        self.copy(ref, ref, n, self.place.sibling()).wait_recv()
-
-    def left(self, ref, n):
-        self.copy(ref, ref, n, self.place.sibling()).wait_send()
-
-
-GATHER_SEMS = 36
+    def start(self, src, dst, out, into, device):
+        self.copy(src, dst, out, into, device).start()
+
+    def arrived(self, ref, into):
+        self.copy(ref, ref, 0, into, self.place.sibling()).wait_recv()
+
+    def left(self, ref, out):
+        self.copy(ref, ref, out, 0, self.place.sibling()).wait_send()
+
+
+GATHER_SEMS = (3, 13)
 ORDER = (0, -1, 1, 2)
 
 
 class Gather(Copies):
-    def __init__(self, place, buffer, send_sems, recv_sems):
+    def __init__(self, place, buffer, direct, send_sems, recv_sems):
         super().__init__(place, send_sems, recv_sems)
-        self.buffer = buffer
+        self.buffer, self.direct = buffer, direct
 
     def block(self, i, j, half=None):
         x, z = self.place.chip(i, j)
         ref = self.buffer.at[x, z, self.place.c]
         return ref if half is None else ref.at[pl.ds(half * 16, 16)]
 
-    def forward(self, ref, n, device):
-        self.start(ref, ref, n, device)
+    def forward(self, ref, out, into, device):
+        self.start(ref, ref, out, into, device)
 
     def to_second(self, i):
-        self.forward(self.block(i, 0), 4 + 4 * (i % 4), self.place.along_z(1))
-        self.forward(self.block(i, 0), 5 + 4 * (i % 4), self.place.along_z(-1))
+        k = 3 + 2 * (i % 4)
+        self.forward(self.block(i, 0), 1, k, self.place.along_z(1))
+        self.forward(self.block(i, 0), 1, k + 1, self.place.along_z(-1))
+        if self.direct:
+            self.forward(self.block(i, 0, 0), 1, 11, self.place.along_z(2))
+            self.forward(self.block(i, 0, 1), 1, 11, self.place.along_z(-2))
         self.to_sibling(i, 0)
 
     def to_sibling(self, i, j):
-        self.forward(self.block(i, j), 20 + 4 * (i % 4) + (j % 4), self.place.sibling())
+        self.forward(self.block(i, j), 2, 12, self.place.sibling())
 
     def stage0(self):
-        self.forward(self.block(0, 0), 0, self.place.along_x(1))
-        self.forward(self.block(0, 0), 1, self.place.along_x(-1))
+        self.forward(self.block(0, 0), 0, 0, self.place.along_x(1))
+        self.forward(self.block(0, 0), 0, 1, self.place.along_x(-1))
+        self.forward(self.block(0, 0, 0), 0, 2, self.place.along_x(2))
+        self.forward(self.block(0, 0, 1), 0, 2, self.place.along_x(-2))
         self.to_second(0)
 
     def stage1(self):
         self.arrived(self.block(-1, 0), 0)
-        self.forward(self.block(-1, 0, 0), 2, self.place.along_x(1))
+        self.to_second(-1)
         self.arrived(self.block(1, 0), 1)
-        self.forward(self.block(1, 0, 1), 3, self.place.along_x(-1))
-        self.to_second(-1)
         self.to_second(1)
 
     def stage2(self):
-        self.arrived(self.block(2, 0, 0), 2)
-        self.arrived(self.block(2, 0, 1), 3)
+        self.arrived(self.block(2, 0), 2)
         self.to_second(2)
 
     def stage3(self):
         for i in ORDER:
-            k = i % 4
-            self.arrived(self.block(i, -1), 4 + 4 * k)
-            self.forward(self.block(i, -1, 0), 6 + 4 * k, self.place.along_z(1))
+            k = 3 + 2 * (i % 4)
+            self.arrived(self.block(i, -1), k)
+            if not self.direct:
+                self.forward(self.block(i, -1, 0), 1, 11, self.place.along_z(1))
             self.to_sibling(i, -1)
-            self.arrived(self.block(i, 1), 5 + 4 * k)
-            self.forward(self.block(i, 1, 1), 7 + 4 * k, self.place.along_z(-1))
+            self.arrived(self.block(i, 1), k + 1)
+            if not self.direct:
+                self.forward(self.block(i, 1, 1), 1, 11, self.place.along_z(-1))
             self.to_sibling(i, 1)
 
     def stage4(self):
+        self.arrived(self.buffer.at[0, :, 0], 11)
         for i in ORDER:
-            k = i % 4
-            self.arrived(self.block(i, 2, 0), 6 + 4 * k)
-            self.arrived(self.block(i, 2, 1), 7 + 4 * k)
             self.to_sibling(i, 2)
 
     def stage5(self):
-        for i in range(4):
-            for j in range(4):
-                x, z = self.place.chip(j, i)
-                self.arrived(self.buffer.at[x, z, 1 - self.place.c], 20 + 4 * i + j)
+        self.arrived(self.buffer.at[:, :, 1 - self.place.c], 12)
 
     def drain(self):
-        whole, half = self.block(0, 0), self.block(0, 0, 0)
-        for n in range(GATHER_SEMS):
-            self.left(half if n in (2, 3) or (n < 20 and n % 4 > 1) else whole, n)
-
-
-REDUCE_SEMS = 21
+        self.left(self.buffer.at[0, pl.ds(0, 3), 0], 0)
+        self.left(self.buffer.at[pl.ds(0, 3), :, 0], 1)
+        self.left(self.buffer.at[:, :, 0], 2)
+
+
+REDUCE_SEMS = (5, 8)
 
 
 def reduce_shapes(half):
@@ -216,17 +216,16 @@
         def _():
             for d1 in (2, 1, 3, 0):
                 src = self.term.at[:, :, 0, (at.y + d1) % 4]
-                self.start(src, self.R.at[d1], d1, at.sibling())
+                self.start(src, self.R.at[d1], 0, 0 if d1 == 2 else 1, at.sibling())
 
         @pl.when(at.c == 0)
         def _():
             for d1 in (2, 1, 3, 0):
                 src = self.term.at[(at.x + d1) % 4, :, 1]
-                self.start(src, self.R.at[d1], d1, at.sibling())
+                self.start(src, self.R.at[d1], 0, 0 if d1 == 2 else 1, at.sibling())
 
     def pair(self, d1):
         at = self.place
-        self.arrived(self.R.at[d1], d1)
         for d2 in range(4):
             x, y = at.quarter(d1, d2)
             for z in range(4):
@@ -237,77 +236,70 @@
 
     def stage1(self):
         at = self.place
+        self.arrived(self.R.at[2], 0)
         self.pair(2)
-        self.start(self.A.at[2, pl.ds(0, 2)], self.T.at[0], 4, at.first(1))
-        self.start(self.A.at[2, pl.ds(2, 2)], self.T.at[1], 5, at.first(-1))
+        self.start(self.A.at[2, pl.ds(0, 2)], self.T.at[0], 1, 2, at.first(1))
+        self.start(self.A.at[2, pl.ds(2, 2)], self.T.at[1], 1, 3, at.first(-1))
+        self.arrived(self.R.at[pl.ds(0, 3)], 1)
         self.pair(1)
         self.pair(3)
         self.pair(0)
 
     def stage2(self):
         at = self.place
-        self.arrived(self.T.at[0], 4)
+        self.arrived(self.T.at[0], 2)
         self.A[1, 0:2] = (self.A[1, 0:2].astype(F32) + self.T[0].astype(F32)).astype(BF16)
-        self.start(self.A.at[1], self.U.at[0], 6, at.first(1))
-        self.arrived(self.T.at[1], 5)
+        self.start(self.A.at[1], self.U.at[0], 1, 4, at.first(1))
+        self.arrived(self.T.at[1], 3)
         self.A[3, 2:4] = (self.A[3, 2:4].astype(F32) + self.T[1].astype(F32)).astype(BF16)
-        self.start(self.A.at[3], self.U.at[1], 7, at.first(-1))
+        self.start(self.A.at[3], self.U.at[1], 1, 4, at.first(-1))
 
     def stage3(self):
         at = self.place
-        self.arrived(self.U.at[0], 6)
-        self.arrived(self.U.at[1], 7)
+        self.arrived(self.U, 4)
         for d2 in (2, 1, 3, 0):
             total = self.A[0, d2].astype(F32) + self.U[0, d2].astype(F32)
             self.B[d2] = (total + self.U[1, d2].astype(F32)).astype(BF16)
             if d2:
-                self.start(self.B.at[d2], self.Y.at[d2 - 1], 7 + d2, at.second(d2))
+                self.start(self.B.at[d2], self.Y.at[d2 - 1], 2, 5, at.second(d2))
 
     def stage4(self):
         at = self.place
-        for d2 in (1, 3, 2):
-            self.arrived(self.Y.at[d2 - 1], 7 + d2)
+        self.arrived(self.Y, 5)
         total = self.B[0].astype(F32) + self.Y[0].astype(F32)
         total = total + self.Y[1].astype(F32) + self.Y[2].astype(F32)
         self.C[...] = total.astype(BF16)
         for d in (4, 3, 5, 2, 6, 1, 7):
-            self.start(self.C.at[(at.zlo + d) % 4], self.V.at[at.z], 10 + d, at.at(dz=d))
+            self.start(self.C.at[(at.zlo + d) % 4], self.V.at[at.z], 3, 6, at.at(dz=d))
         self.V[at.z] = self.C[at.zlo]
 
     def stage5(self):
         at = self.place
-        for d in (1, 7, 2, 6, 3, 5, 4):
-            self.arrived(self.V.at[(at.z + 8 - d) % 8], 10 + d)
+        self.arrived(self.V.at[pl.ds(0, 7)], 6)
         total = self.V[0].astype(F32)
         for z in range(1, 8):
             total = total + self.V[z].astype(F32)
         self.E[...] = total.astype(BF16)
         for d in (2, 1, 3):
-            self.start(self.E, self.O.at[at.y], 17 + d, at.at(dy=d))
+            self.start(self.E, self.O.at[at.y], 4, 7, at.at(dy=d))
 
     def stage6(self, write):
         at = self.place
-        for d in (1, 3, 2):
-            self.arrived(self.O.at[(at.y - d + 4) % 4], 17 + d)
+        self.arrived(self.O.at[pl.ds(0, 3)], 7)
         self.O[at.y] = self.E[...]
         for r in range(2):
             for k in range(2):
                 write(r, k, self.O[2 * r + k])
 
     def drain(self):
-        for d1 in range(4):
-            self.left(self.R.at[d1], d1)
-        self.left(self.T.at[0], 4)
-        self.left(self.T.at[1], 5)
-        self.left(self.U.at[0], 6)
-        self.left(self.U.at[1], 7)
-        for d2 in (1, 2, 3):
-            self.left(self.B.at[0], 7 + d2)
-        for n in range(11, 21):
-            self.left(self.E, n)
-
-
-SMALL_SEMS = 14
+        self.left(self.R, 0)
+        self.left(self.A.at[pl.ds(0, 3)], 1)
+        self.left(self.A.at[0, pl.ds(0, 3)], 2)
+        self.left(self.V.at[pl.ds(0, 7)], 3)
+        self.left(self.O.at[pl.ds(0, 3)], 4)
+
+
+SMALL_SEMS = (4, 4)
 
 
 class Small(Copies):
@@ -317,24 +309,23 @@
 
     def step(self, n):
         at = self.place
-        size, mine, first = ((4, at.x, 0), (4, at.y, 3), (8, at.z, 6), (2, at.c, 13))[n]
+        size, mine = ((4, at.x), (4, at.y), (8, at.z), (2, at.c))[n]
         other = (
             lambda d: at.at(dx=d),
             lambda d: at.at(dy=d),
             lambda d: at.at(dz=d),
             lambda d: at.sibling(),
         )[n]
-        return size, mine, first, other
+        return size, mine, other
 
     def send(self, n):
-        size, mine, first, other = self.step(n)
+        size, mine, other = self.step(n)
         for d in range(1, size):
-            self.start(self.tile.at[n], self.slots.at[n, mine], first + d - 1, other(d))
+            self.start(self.tile.at[n], self.slots.at[n, mine], n, n, other(d))
 
     def receive(self, n):
-        size, mine, first, _ = self.step(n)
-        for d in range(1, size):
-            self.arrived(self.slots.at[n, (mine - d + size) % size], first + d - 1)
+        size, mine, _ = self.step(n)
+        self.arrived(self.slots.at[n, pl.ds(0, size - 1)], n)
         self.slots[n, mine] = self.tile[n]
         total = self.slots[n, 0].astype(F32)
         for k in range(1, size):
@@ -360,39 +351,39 @@
         write(self.receive(3))
 
     def drain(self):
-        for n in range(SMALL_SEMS):
-            self.left(self.tile.at[0], n)
+        for n in range(4):
+            self.left(self.slots.at[n, pl.ds(0, self.step(n)[0] - 1)], n)
 
 
 class Timeline:
     def __init__(self):
         self.now, self.live = 0.0, []
 
-    def add(self, stages):
-        work = [self.now, len(self.live), list(stages)]
+    def add(self, stages, start=0.0, first=0.0):
+        work = [max(start, self.now), first, len(self.live), list(stages)]
         self.live.append(work)
         self.run(self.now)
         return work
 
     def step(self, work):
-        call, latency = work[2].pop(0)
+        call, latency = work[3].pop(0)
         call()
         work[0] = max(self.now, work[0]) + latency
 
     def run(self, until):
         while True:
-            ready = [w for w in self.live if w[2] and w[0] <= until]
+            ready = [w for w in self.live if w[3] and w[0] <= until]
             if not ready:
                 return
-            self.step(min(ready, key=lambda w: (w[0], w[1])))
+            self.step(min(ready, key=lambda w: (w[0] - w[1], w[2])))
 
     def spend(self, time):
         self.now += time
         self.run(self.now)
 
     def finish(self, work):
-        while work[2]:
-            self.now = max(self.now, min(w[0] for w in self.live if w[2]))
+        while work[3]:
+            self.now = max(self.now, min(w[0] for w in self.live if w[3]))
             self.run(self.now)
 
 
@@ -413,6 +404,8 @@
     "low": ((2, 384, 384), BF16),
     "dscores": ((2, 384, 384), BF16),
     "gh": ((384, 1024), F32),
+    "tokens": ((384, 1024), BF16),
+    "cot": ((384, 1024), BF16),
     "own": ((128, 128), F32),
     "own_low": ((32, 128), BF16),
     "sums": ((16, 128), F32),
@@ -426,8 +419,8 @@
     S["own_low"][...] = S["own"][...].T[0:32].astype(BF16)
 
 
-def prologue_tokens(S, tok_ref, cot_ref, count_ref, starts_ref):
-    source = tok_ref[...].astype(F32)
+def prologue_tokens(S, count_ref, starts_ref):
+    source = S["tokens"][...].astype(F32)
     center = jnp.mean(source, axis=1, keepdims=True)
     centered = source - center
     variance = jnp.mean(centered * centered, axis=1, keepdims=True)
@@ -449,11 +442,11 @@
     alive = lax.broadcasted_iota(jnp.int32, (ROWS, 128), 0) < count
     S["live"][...] = jnp.where(alive, 1.0, 0.0).astype(F32)
     alive = S["live"][:, 0:1] > 0.5
-    S["mcot"][...] = jnp.where(alive, cot_ref[...].astype(F32), 0.0).astype(BF16)
+    S["mcot"][...] = jnp.where(alive, S["cot"][...].astype(F32), 0.0).astype(BF16)
 
 
 def prologue_hidden(S):
-    small = S["Wps"][:, :, :, :, 1024:1152].reshape(1024, 128).astype(F32)
+    small = S["W0"][:, :, :, :, 768:896].reshape(1024, 128).astype(F32)
     S["gains"][...] = small.T[0:2, :]
     gain = S["gains"][0:1, :]
     shift = S["gains"][1:2, :]
@@ -463,7 +456,7 @@
 
 def grads_attended(S):
     for g in range(4):
-        part = S["Wps"][g, :, :, :, 0:1024].reshape(256, 1024)
+        part = S["Wp"][g].reshape(256, 1024)
         S["ga"][g] = nt(S["mcot"][...], part).astype(BF16)
 
 
@@ -480,7 +473,7 @@
 def forward(S, g, spend):
     qkv, slot = S["qkv"].at[g % 2], g % 2
     for n in range(3):
-        weight = S["Wg"][g, :, :, :, :, n * 256 : n * 256 + 256].reshape(1024, 256)
+        weight = S[f"W{g}"][:, :, :, :, n * 256 : n * 256 + 256].reshape(1024, 256)
         part = nn(S["hidden"][...], weight).astype(BF16)
         qkv[:, n * 256 : n * 256 + 256] = part * jnp.asarray(0.125, BF16) if n == 0 else part
     spend(0.9)
@@ -519,8 +512,10 @@
         spend(0.8)
 
 
-def weight_grads(S, g):
+def weight_grads(S, g, spend):
     for m in range(4):
+        if m:
+            spend(0.25)
         part = nn(S["hidden_t"][m * 256 : m * 256 + 256], S["dqkv"][...]).astype(BF16)
         part = part.reshape(4, 2, 2, 16, 768)
         for r in range(2):
@@ -528,11 +523,12 @@
                 S["G"][g, m, :, :, 2 * r + k] = part[:, :, r, :, k * 384 : k * 384 + 384]
 
 
-def hidden_grads(S, g):
+def hidden_grads(S, g, spend):
     for n in range(4):
-        part = nt(S["dqkv"][...], S["Wg"][g, n].reshape(256, 768))
+        part = nt(S["dqkv"][...], S[f"W{g}"][n, :, :, :, 0:768].reshape(256, 768))
         columns = slice(n * 256, n * 256 + 256)
         S["gh"][:, columns] = part if g == 0 else S["gh"][:, columns] + part
+        spend(0.2)
 
 
 def proj_grads(S):
@@ -558,7 +554,7 @@
     grad_normed = S["gh"][...] * S["gains"][0:1, :]
     inner = grad_normed - jnp.mean(grad_normed, axis=1, keepdims=True)
     inner = inner - normed * jnp.mean(grad_normed * normed, axis=1, keepdims=True)
-    S["gh"][...] = S["inverse"][:, 0:1] * inner
+    S["tokens"][...] = (S["cot"][...].astype(F32) + S["inverse"][:, 0:1] * inner).astype(BF16)
 
 
 COMM = {}
@@ -566,8 +562,9 @@
     COMM["g_" + _name] = ((4,) + _shape, BF16)
 for _name, _shape in reduce_shapes(512).items():
     COMM["p_" + _name] = (_shape, BF16)
-COMM["Wg"] = ((4, 4, 4, 2, 32, 768), BF16)
-COMM["Wps"] = ((4, 4, 2, 32, 1152), BF16)
+for _g, _width in enumerate((896, 768, 768, 768)):
+    COMM[f"W{_g}"] = ((4, 4, 2, 32, _width), BF16)
+COMM["Wp"] = ((4, 4, 2, 32, 1024), BF16)
 COMM["G"] = ((4, 4, 4, 2, 4, 16, 384), BF16)
 COMM["Gp"] = ((4, 4, 2, 4, 16, 512), BF16)
 COMM["tile"] = ((4, 16, 128), BF16)
@@ -596,37 +593,40 @@
     x, z, c = place.x, place.zlo, place.c
     time = Timeline()
 
-    own_small(S, gain_ref, shift_ref)
-    local = []
-    for n, (src, dst) in enumerate(
-        [
-            (proj_ref, S["Wps"].at[x, z, c, :, pl.ds(0, 1024)]),
-            (S["own_low"], S["Wps"].at[x, z, c, :, pl.ds(1024, 128)]),
-        ]
-        + [
-            (
-                qkv_ref.at[:, pl.ds(part * 1024 + g * 256, 256)],
-                S["Wg"].at[g, x, z, c, :, pl.ds(part * 256, 256)],
-            )
-            for g in range(4)
-            for part in range(3)
-        ]
-    ):
-        copy = pltpu.make_async_copy(src, dst, ls.at[n])
-        copy.start()
-        local.append(copy)
-
-    enter(place.all(), lambda: prologue_tokens(S, tok_ref, cot_ref, count_ref, starts_ref))
-    for copy in local:
-        copy.wait()
-
-    buffers = [S["Wps"]] + [S["Wg"].at[g] for g in range(4)]
-    gathers = [Gather(place, b, gs.at[k], gr.at[k]) for k, b in enumerate(buffers)]
-
-    def gather(k):
+    def prepare():
+        into = [(tok_ref, S["tokens"]), (cot_ref, S["cot"]), (proj_ref, S["Wp"].at[x, z, c])]
+        into = [pltpu.make_async_copy(a, b, ls.at[n]) for n, (a, b) in enumerate(into)]
+        for copy in into:
+            copy.start()
+        for g in range(4):
+            for part in range(3):
+                pltpu.make_async_copy(
+                    qkv_ref.at[:, pl.ds(part * 1024 + g * 256, 256)],
+                    S[f"W{g}"].at[x, z, c, :, pl.ds(part * 256, 256)],
+                    ls.at[3 + g],
+                ).start()
+        own_small(S, gain_ref, shift_ref)
+        last = S["W0"].at[x, z, c, :, pl.ds(768, 128)]
+        last = pltpu.make_async_copy(S["own_low"], last, ls.at[7])
+        last.start()
+        into[0].wait()
+        into[1].wait()
+        prologue_tokens(S, count_ref, starts_ref)
+        into[2].wait()
+        last.wait()
+        for g in range(4):
+            own = S[f"W{g}"].at[x, z, c, :, pl.ds(0, 768)]
+            pltpu.make_async_copy(own, own, ls.at[3 + g]).wait()
+
+    enter(place.all(), prepare)
+
+    buffers = [S[f"W{g}"] for g in range(4)] + [S["Wp"]]
+    gathers = [Gather(place, b, k in DIRECT, gs.at[k], gr.at[k]) for k, b in enumerate(buffers)]
+
+    def gather(k, start):
         piece = gathers[k]
         calls = (piece.stage0, piece.stage1, piece.stage2, piece.stage3, piece.stage4, piece.stage5)
-        return time.add(zip(calls, GATHER_TIMES))
+        return time.add(zip(calls, DIRECT_TIMES if piece.direct else GATHER_TIMES), start)
 
     def write_group(g):
         def write(r, k, value):
@@ -660,42 +660,40 @@
         reduces.append(piece)
         calls = (piece.stage0, piece.stage1, piece.stage2, piece.stage3, piece.stage4)
         calls += (piece.stage5, functools.partial(piece.stage6, write))
-        return time.add(zip(calls, REDUCE_TIMES))
-
-    works = []
-    for k in GATHER_ORDER:
-        works.append((k, gather(k)))
-        time.now += GATHER_GAP
-    works = [w for _, w in sorted(works, key=lambda pair: pair[0])]
-    time.now = 0.0
+        return time.add(zip(calls, REDUCE_TIMES), 0.0, 1.5 if sem == 3 else 0.0)
+
+    works = dict((k, gather(k, start)) for k, start in GATHER_STARTS)
     time.finish(works[0])
     prologue_hidden(S)
-    time.spend(1.0)
-    time.finish(works[1])
+    time.spend(0.5)
     forward(S, 0, time.spend)
+    time.finish(works[4])
     grads_attended(S)
     time.spend(1.0)
     for g in range(4):
-        if g < 3:
-            time.finish(works[g + 2])
+        if 0 < g < 3:
+            time.finish(works[g + 1])
             forward(S, g + 1, time.spend)
-            if g == 2:
-                proj_grads(S)
-                reduce(S["Gp"], [S["p_" + n] for n in REDUCE_NAMES], 4, write_proj)
+        if g == 2:
+            proj_grads(S)
+            reduce(S["Gp"], [S["p_" + n] for n in REDUCE_NAMES], 4, write_proj)
+            time.spend(1.3)
         backward(S, g, time.spend)
-        weight_grads(S, g)
+        weight_grads(S, g, time.spend)
         names = [S["g_" + n].at[g] for n in REDUCE_NAMES]
         reduce(S["G"].at[g], names, g, write_group(g))
-        time.spend(0.8)
-        hidden_grads(S, g)
-        time.spend(1.0)
+        hidden_grads(S, g, time.spend)
+        if g == 0:
+            time.finish(works[1])
+            forward(S, 1, time.spend)
     small_grads(S)
     small = Small(place, S["tile"], S["slots"], ss, sr)
     calls = (small.stage0, small.stage1, small.stage2, small.stage3)
     calls += (functools.partial(small.stage4, write_small),)
     time.add(zip(calls, SMALL_TIMES))
+    time.spend(0.3)
     token_grads(S)
-    out = pltpu.make_async_copy(S["gh"], out_ref, ls.at[0])
+    out = pltpu.make_async_copy(S["tokens"], out_ref, ls.at[0])
     out.start()
     time.spend(0.8)
     for work in list(time.live):
@@ -705,11 +703,52 @@
         piece.drain()
 
 
-GATHER_ORDER = (0, 1, 2, 3, 4)
-GATHER_GAP = 3.0
-GATHER_TIMES = (3.0, 3.0, 3.0, 4.0, 2.5, 0.0)
-REDUCE_TIMES = (2.5, 3.0, 4.0, 3.5, 4.0, 3.0, 0.0)
-SMALL_TIMES = (2.5, 2.5, 4.0, 1.5, 0.0)
+GATHER_STARTS = ((0, 0.0), (4, 3.4), (1, 8.0), (2, 11.5), (3, 15.0))
+DIRECT = (0, 4)
+DIRECT_TIMES = (3.4, 0.8, 6.0, 0.9, 2.0, 0.0)
+GATHER_TIMES = (3.6, 0.8, 4.5, 4.0, 2.0, 0.0)
+REDUCE_TIMES = (2.5, 4.5, 5.0, 4.5, 4.8, 30.0, 0.0)
+SMALL_TIMES = (4.3, 5.3, 5.3, 30.0, 0.0)
+
+
+LAST_SHAPES = (
+    (ROWS, D, BF16, BF16),
+    (32, 3072, BF16, F32),
+    (32, 1024, BF16, F32),
+    (1, 32, F32, F32),
+    (1, 32, F32, F32),
+)
+
+
+def last_kernel(scale, *refs):
+    ins, outs, scratch, sems = refs[:5], refs[5:10], refs[10:-1], refs[-1]
+    before = scratch[:5]
+    after = (scratch[0],) + scratch[5:]
+    into = [pltpu.make_async_copy(a, b, sems.at[n]) for n, (a, b) in enumerate(zip(ins, before))]
+    out = [pltpu.make_async_copy(a, b, sems.at[5 + n]) for n, (a, b) in enumerate(zip(after, outs))]
+    for copy in into:
+        copy.start()
+    for n in (1, 2, 3, 4, 0):
+        into[n].wait()
+        if n:
+            after[n][...] = before[n][...].astype(F32) * scale
+        out[n].start()
+    for copy in out:
+        copy.wait()
+
+
+def last(scale, *arrays):
+    anyspace = pl.BlockSpec(memory_space=pl.ANY)
+    return pl.pallas_call(
+        functools.partial(last_kernel, scale),
+        out_shape=[jax.ShapeDtypeStruct((r, c), t) for r, c, _, t in LAST_SHAPES],
+        in_specs=[anyspace] * 5,
+        out_specs=[anyspace] * 5,
+        scratch_shapes=[pltpu.VMEM((r, c), t) for r, c, t, _ in LAST_SHAPES]
+        + [pltpu.VMEM((r, c), t) for r, c, _, t in LAST_SHAPES[1:]]
+        + [pltpu.SemaphoreType.DMA((10,))],
+        name="last",
+    )(*arrays)
 
 
 def fused(counts, starts, tokens, cotangent, qkv_weight, proj_weight, gain, shift):
@@ -720,23 +759,23 @@
     return pl.pallas_call(
         kernel,
         out_shape=[
-            jax.ShapeDtypeStruct((ROWS, D), F32),
+            jax.ShapeDtypeStruct((ROWS, D), BF16),
             jax.ShapeDtypeStruct((32, 3072), BF16),
             jax.ShapeDtypeStruct((32, 1024), BF16),
             jax.ShapeDtypeStruct((1, 32), F32),
             jax.ShapeDtypeStruct((1, 32), F32),
         ],
-        in_specs=[smem, smem, vmem, vmem, anyspace, anyspace, vmem, vmem],
+        in_specs=[smem, smem] + [anyspace] * 4 + [vmem] * 2,
         out_specs=[anyspace] + [vmem] * 4,
         scratch_shapes=[pltpu.VMEM(*b) for b in buffers]
         + [
-            pltpu.SemaphoreType.DMA((5, GATHER_SEMS)),
-            pltpu.SemaphoreType.DMA((5, GATHER_SEMS)),
-            pltpu.SemaphoreType.DMA((5, REDUCE_SEMS)),
-            pltpu.SemaphoreType.DMA((5, REDUCE_SEMS)),
-            pltpu.SemaphoreType.DMA((SMALL_SEMS,)),
-            pltpu.SemaphoreType.DMA((SMALL_SEMS,)),
-            pltpu.SemaphoreType.DMA((14,)),
+            pltpu.SemaphoreType.DMA((5, GATHER_SEMS[0])),
+            pltpu.SemaphoreType.DMA((5, GATHER_SEMS[1])),
+            pltpu.SemaphoreType.DMA((5, REDUCE_SEMS[0])),
+            pltpu.SemaphoreType.DMA((5, REDUCE_SEMS[1])),
+            pltpu.SemaphoreType.DMA((SMALL_SEMS[0],)),
+            pltpu.SemaphoreType.DMA((SMALL_SEMS[1],)),
+            pltpu.SemaphoreType.DMA((8,)),
         ],
         compiler_params=pltpu.CompilerParams(
             collective_id=0, has_side_effects=True, vmem_limit_bytes=67043328
@@ -750,7 +789,7 @@
 ):
     everyone = lax.axis_size("dp") * lax.axis_size("fsdp")
     scale = 1.0 / math.sqrt(tokens.shape[0] * everyone)
-    through_norm, qkv_grad, proj_grad, gain_grad, shift_grad = fused(
+    sums = fused(
         patch_count,
         image_starts,
         tokens,
@@ -760,13 +799,8 @@
         norm_gain.reshape(1, -1),
         norm_shift.reshape(1, -1),
     )
-    return (
-        (cotangent.astype(F32) + through_norm).astype(BF16),
-        qkv_grad.astype(F32) * scale,
-        proj_grad.astype(F32) * scale,
-        gain_grad.reshape(-1) * scale,
-        shift_grad.reshape(-1) * scale,
-    )
+    grad_block, qkv_grad, proj_grad, gain_grad, shift_grad = last(scale, *sums)
+    return (grad_block, qkv_grad, proj_grad, gain_grad.reshape(-1), shift_grad.reshape(-1))
 
 
 def solution(mesh):

time: 115 us -> 96.4 us (0.84)
  Pallas kernels: 108 us -> 94.4 us
  other arithmetic: 4.75 us -> 0 us
    pallas_call x1 -> x2, Pallas kernels: 108 us -> 94.4 us  [the longest x1 92 us: fused(): pl.pallas_call(kernel, out_shape=[jax.ShapeDtypeStruct((ROWS, D), BF16),...]
    convert_element_type x1 -> x0, other arithmetic: 2.78 us -> none  [per_device(): (cotangent.astype(F32) + through_norm).astype(BF16)]
    mul x3 -> x0, other arithmetic: 1.96 us -> none  [the longest x1 0.78 us: per_device(): qkv_grad.astype(F32) * scale]
where the time goes in v4:
time: 96.4 us; the launch traced here: 95.9 us
  Pallas kernels  94.4 us (98%)
  between operations  1.47 us (2%)
    pallas_call x1, Pallas kernels, fused(): pl.pallas_call(kernel, out_shape=[jax.ShapeDtypeStruct((ROWS, D), BF16),...  92 us
    pallas_call x1, Pallas kernels, last(): pl.pallas_call(functools.partial(last_kernel, scale), out_shape=[jax.Shap...  2.35 us

profile of v4, /device:TPU:32, one launch (start us, length us, event | category | flops | bytes accessed | tf_op | source)
XLA Modules:
  0.0 95.9 jit_solution(15149823903913323006)
XLA Ops:
  1.3 92.0 %fused.1 = (bf16[384,1024]{1,0:T(8,128)(2,1)}, bf16[32,3072]{1,0:T(8,128)(2,1)}, bf16[32,1024]{1,0:T(8,128)(2,1)}, f32[1,32]{1,0:T(1,128)}, f32[1,32]{1,0:T(1,128)}) custom-call(s32[1]{0:T(128)S(6)} %copy.13.count_ref, s32[1,8]{1,0:T(1,128)} %starts_ref.1, bf16[384,1024]{1,0:T(8,128)(2,1)} %tok_ref.1, bf16[384,1024]{1,0:T(8,128)(2,1)} %cot_ref.1, ...), custom_call_target="tpu_custom_call" | custom-call | tf_op jit(solution)/shard_map/fused/pallas_call | solution.py:759
  93.3 2.3 %last.1 = (bf16[384,1024]{1,0:T(8,128)(2,1)}, f32[32,3072]{1,0:T(8,128)}, f32[32,1024]{1,0:T(8,128)}, f32[1,32]{1,0:T(1,128)}, f32[1,32]{1,0:T(1,128)}) custom-call(bf16[384,1024]{1,0:T(8,128)(2,1)} %get-tuple-element.15.refs_0_, bf16[32,3072]{1,0:T(8,128)(2,1)} %get-tuple-element.16.refs_1_, bf16[32,1024]{1,0:T(8,128)(2,1)} %get-tuple-element.17.refs_2_, ...), custom_call_target="tpu_custom_call" | custom-call | tf_op jit(solution)/shard_map/last/pallas_call | solution.py:742

commit v5 on v4

--- a/solution.py
+++ b/solution.py
@@ -242,17 +242,23 @@
         self.start(self.A.at[2, pl.ds(2, 2)], self.T.at[1], 1, 3, at.first(-1))
         self.arrived(self.R.at[pl.ds(0, 3)], 1)
         self.pair(1)
+        self.give(0, 1, 2, at.first(1))
         self.pair(3)
+        self.give(1, 3, 0, at.first(-1))
         self.pair(0)
+
+    def give(self, slot, d1, d2, device):
+        half = pl.ds(d2, 2)
+        self.start(self.A.at[d1, half], self.U.at[slot, half], 1, 4, device)
 
     def stage2(self):
         at = self.place
         self.arrived(self.T.at[0], 2)
         self.A[1, 0:2] = (self.A[1, 0:2].astype(F32) + self.T[0].astype(F32)).astype(BF16)
-        self.start(self.A.at[1], self.U.at[0], 1, 4, at.first(1))
+        self.give(0, 1, 0, at.first(1))
         self.arrived(self.T.at[1], 3)
         self.A[3, 2:4] = (self.A[3, 2:4].astype(F32) + self.T[1].astype(F32)).astype(BF16)
-        self.start(self.A.at[3], self.U.at[1], 1, 4, at.first(-1))
+        self.give(1, 3, 2, at.first(-1))
 
     def stage3(self):
         at = self.place
@@ -397,7 +403,7 @@
     "ga": ((4, 384, 256), BF16),
     "att": ((4, 384, 256), BF16),
     "qkv": ((2, 384, 768), BF16),
-    "dqkv": ((384, 768), BF16),
+    "dqkv": ((4, 384, 768), BF16),
     "bias": ((384, 384), F32),
     "gains": ((2, 1024), F32),
     "probs": ((2, 4, 384, 384), F32),
@@ -409,13 +415,15 @@
     "own": ((128, 128), F32),
     "own_low": ((32, 128), BF16),
     "sums": ((16, 128), F32),
+    "gain": ((1, 32), BF16),
+    "shift": ((1, 32), BF16),
 }
 
 
-def own_small(S, gain_ref, shift_ref):
+def own_small(S):
     S["own"][...] = jnp.zeros((128, 128), F32)
-    S["own"][0:1, 0:32] = gain_ref[...].astype(F32)
-    S["own"][1:2, 0:32] = shift_ref[...].astype(F32)
+    S["own"][0:1, 0:32] = S["gain"][...].astype(F32)
+    S["own"][1:2, 0:32] = S["shift"][...].astype(F32)
     S["own_low"][...] = S["own"][...].T[0:32].astype(BF16)
 
 
@@ -476,7 +484,7 @@
         weight = S[f"W{g}"][:, :, :, :, n * 256 : n * 256 + 256].reshape(1024, 256)
         part = nn(S["hidden"][...], weight).astype(BF16)
         qkv[:, n * 256 : n * 256 + 256] = part * jnp.asarray(0.125, BF16) if n == 0 else part
-    spend(0.9)
+    spend(0.8)
     for pair in range(2):
         q2, k2, v2 = (lanes(qkv, pair, n) for n in range(3))
         for h in range(2):
@@ -488,7 +496,7 @@
             S["low"][h] = probs.astype(BF16)
         att = sum(nn(S["low"][h], own(v2, h)) for h in range(2))
         S["att"][g, :, pair * 128 : pair * 128 + 128] = att.astype(BF16)
-        spend(1.0)
+        spend(0.85)
 
 
 def backward(S, g, spend):
@@ -502,33 +510,33 @@
             delta = jnp.sum(probs * grad_probs, axis=1, keepdims=True)
             S["dscores"][h] = (probs * (grad_probs - delta)).astype(BF16)
             S["low"][h] = probs.astype(BF16)
-        spend(0.8)
+        spend(0.55)
         dv = sum(tn(S["low"][h], own(o2, h)) for h in range(2))
         dq = sum(nn(S["dscores"][h], own(k2, h)) for h in range(2)) * 0.125
         dk = sum(tn(S["dscores"][h], own(q2, h)) for h in range(2))
         for n, part in enumerate((dq, dk, dv)):
             start = n * 256 + pair * 128
-            S["dqkv"][:, start : start + 128] = part.astype(BF16)
-        spend(0.8)
+            S["dqkv"][g, :, start : start + 128] = part.astype(BF16)
+        spend(0.55)
 
 
 def weight_grads(S, g, spend):
     for m in range(4):
         if m:
             spend(0.25)
-        part = nn(S["hidden_t"][m * 256 : m * 256 + 256], S["dqkv"][...]).astype(BF16)
+        part = nn(S["hidden_t"][m * 256 : m * 256 + 256], S["dqkv"][g]).astype(BF16)
         part = part.reshape(4, 2, 2, 16, 768)
         for r in range(2):
             for k in range(2):
                 S["G"][g, m, :, :, 2 * r + k] = part[:, :, r, :, k * 384 : k * 384 + 384]
 
 
-def hidden_grads(S, g, spend):
+def hidden_grads(S, spend):
     for n in range(4):
-        part = nt(S["dqkv"][...], S[f"W{g}"][n, :, :, :, 0:768].reshape(256, 768))
-        columns = slice(n * 256, n * 256 + 256)
-        S["gh"][:, columns] = part if g == 0 else S["gh"][:, columns] + part
-        spend(0.2)
+        S["gh"][:, n * 256 : n * 256 + 256] = sum(
+            nt(S["dqkv"][g], S[f"W{g}"][n, :, :, :, 0:768].reshape(256, 768)) for g in range(4)
+        )
+        spend(1.15)
 
 
 def proj_grads(S):
@@ -588,12 +596,16 @@
     *scratch,
 ):
     S = dict(zip(tuple(SCRATCH) + tuple(COMM), scratch))
-    gs, gr, rs, rr, ss, sr, ls = scratch[len(S) :]
+    gs, gr, rs, rr, ss, sr, ls, count, starts = scratch[len(S) :]
     place = Place()
     x, z, c = place.x, place.zlo, place.c
     time = Timeline()
 
     def prepare():
+        few = (count_ref, count), (starts_ref, starts), (gain_ref, S["gain"]), (shift_ref, S["shift"])
+        few = [pltpu.make_async_copy(a, b, ls.at[8 + n]) for n, (a, b) in enumerate(few)]
+        for copy in few:
+            copy.start()
         into = [(tok_ref, S["tokens"]), (cot_ref, S["cot"]), (proj_ref, S["Wp"].at[x, z, c])]
         into = [pltpu.make_async_copy(a, b, ls.at[n]) for n, (a, b) in enumerate(into)]
         for copy in into:
@@ -605,13 +617,15 @@
                     S[f"W{g}"].at[x, z, c, :, pl.ds(part * 256, 256)],
                     ls.at[3 + g],
                 ).start()
-        own_small(S, gain_ref, shift_ref)
+        for copy in few:
+            copy.wait()
+        own_small(S)
         last = S["W0"].at[x, z, c, :, pl.ds(768, 128)]
         last = pltpu.make_async_copy(S["own_low"], last, ls.at[7])
         last.start()
         into[0].wait()
         into[1].wait()
-        prologue_tokens(S, count_ref, starts_ref)
+        prologue_tokens(S, count, starts)
         into[2].wait()
         last.wait()
         for g in range(4):
@@ -660,7 +674,8 @@
         reduces.append(piece)
         calls = (piece.stage0, piece.stage1, piece.stage2, piece.stage3, piece.stage4)
         calls += (piece.stage5, functools.partial(piece.stage6, write))
-        return time.add(zip(calls, REDUCE_TIMES), 0.0, 1.5 if sem == 3 else 0.0)
+        final = sem == 3
+        return time.add(zip(calls, REDUCE_TIMES[sem]), 0.0, 1.5 if final else 0.0)
 
     works = dict((k, gather(k, start)) for k, start in GATHER_STARTS)
     time.finish(works[0])
@@ -682,15 +697,16 @@
         weight_grads(S, g, time.spend)
         names = [S["g_" + n].at[g] for n in REDUCE_NAMES]
         reduce(S["G"].at[g], names, g, write_group(g))
-        hidden_grads(S, g, time.spend)
+        time.spend(0.25)
         if g == 0:
             time.finish(works[1])
             forward(S, 1, time.spend)
+    hidden_grads(S, time.spend)
     small_grads(S)
     small = Small(place, S["tile"], S["slots"], ss, sr)
     calls = (small.stage0, small.stage1, small.stage2, small.stage3)
     calls += (functools.partial(small.stage4, write_small),)
-    time.add(zip(calls, SMALL_TIMES))
+    time.add(zip(calls, SMALL_TIMES), 0.0, 1.0)
     time.spend(0.3)
     token_grads(S)
     out = pltpu.make_async_copy(S["tokens"], out_ref, ls.at[0])
@@ -707,8 +723,11 @@
 DIRECT = (0, 4)
 DIRECT_TIMES = (3.4, 0.8, 6.0, 0.9, 2.0, 0.0)
 GATHER_TIMES = (3.6, 0.8, 4.5, 4.0, 2.0, 0.0)
-REDUCE_TIMES = (2.5, 4.5, 5.0, 4.5, 4.8, 30.0, 0.0)
-SMALL_TIMES = (4.3, 5.3, 5.3, 30.0, 0.0)
+EARLY = (2.5, 4.8, 5.0, 5.0, 5.5, 30.0, 0.0)
+LATE = (2.0, 4.5, 5.5, 5.5, 5.0, 30.0, 0.0)
+FINAL = (1.5, 4.3, 4.8, 4.2, 4.6, 30.0, 0.0)
+REDUCE_TIMES = (EARLY, EARLY, LATE, FINAL, (4.3,) + LATE[1:])
+SMALL_TIMES = (4.4, 4.6, 5.6, 25.0, 0.0)
 
 
 LAST_SHAPES = (
@@ -754,7 +773,6 @@
 def fused(counts, starts, tokens, cotangent, qkv_weight, proj_weight, gain, shift):
     anyspace = pl.BlockSpec(memory_space=pl.ANY)
     vmem = pl.BlockSpec(memory_space=pltpu.VMEM)
-    smem = pl.BlockSpec(memory_space=pltpu.SMEM)
     buffers = tuple(SCRATCH.values()) + tuple(COMM.values())
     return pl.pallas_call(
         kernel,
@@ -765,7 +783,7 @@
             jax.ShapeDtypeStruct((1, 32), F32),
             jax.ShapeDtypeStruct((1, 32), F32),
         ],
-        in_specs=[smem, smem] + [anyspace] * 4 + [vmem] * 2,
+        in_specs=[anyspace] * 8,
         out_specs=[anyspace] + [vmem] * 4,
         scratch_shapes=[pltpu.VMEM(*b) for b in buffers]
         + [
@@ -775,7 +793,9 @@
             pltpu.SemaphoreType.DMA((5, REDUCE_SEMS[1])),
             pltpu.SemaphoreType.DMA((SMALL_SEMS[0],)),
             pltpu.SemaphoreType.DMA((SMALL_SEMS[1],)),
-            pltpu.SemaphoreType.DMA((8,)),
+            pltpu.SemaphoreType.DMA((12,)),
+            pltpu.SMEM((1,), jnp.int32),
+            pltpu.SMEM((1, 8), jnp.int32),
         ],
         compiler_params=pltpu.CompilerParams(
             collective_id=0, has_side_effects=True, vmem_limit_bytes=67043328

time: 96.4 us -> 91.9 us (0.953)
  Pallas kernels: 94.4 us -> 90.2 us
    pallas_call x1, Pallas kernels: 92 us -> 87.8 us  [fused(): pl.pallas_call(kernel, out_shape=[jax.ShapeDtypeStruct((ROWS, D), BF16),...]
where the time goes in v5:
time: 91.9 us; the launch traced here: 91.6 us
  Pallas kernels  90.2 us (98%)
  between operations  1.47 us (2%)
    pallas_call x1, Pallas kernels, fused(): pl.pallas_call(kernel, out_shape=[jax.ShapeDtypeStruct((ROWS, D), BF16),...  87.8 us
    pallas_call x1, Pallas kernels, last(): pl.pallas_call(functools.partial(last_kernel, scale), out_shape=[jax.Shap...  2.35 us

profile of v5, /device:TPU:32, one launch (start us, length us, event | category | flops | bytes accessed | tf_op | source)
XLA Modules:
  0.0 91.6 jit_solution(14933021186954948970)
XLA Ops:
  1.3 87.8 %fused.1 = (bf16[384,1024]{1,0:T(8,128)(2,1)}, bf16[32,3072]{1,0:T(8,128)(2,1)}, bf16[32,1024]{1,0:T(8,128)(2,1)}, f32[1,32]{1,0:T(1,128)}, f32[1,32]{1,0:T(1,128)}) custom-call(s32[1]{0:T(128)S(6)} %copy.13.count_ref, s32[1,8]{1,0:T(1,128)} %starts_ref.1, bf16[384,1024]{1,0:T(8,128)(2,1)} %tok_ref.1, bf16[384,1024]{1,0:T(8,128)(2,1)} %cot_ref.1, ...), custom_call_target="tpu_custom_call" | custom-call | tf_op jit(solution)/shard_map/fused/pallas_call | solution.py:777
  89.1 2.3 %last.1 = (bf16[384,1024]{1,0:T(8,128)(2,1)}, f32[32,3072]{1,0:T(8,128)}, f32[32,1024]{1,0:T(8,128)}, f32[1,32]{1,0:T(1,128)}, f32[1,32]{1,0:T(1,128)}) custom-call(bf16[384,1024]{1,0:T(8,128)(2,1)} %get-tuple-element.15.refs_0_, bf16[32,3072]{1,0:T(8,128)(2,1)} %get-tuple-element.16.refs_1_, bf16[32,1024]{1,0:T(8,128)(2,1)} %get-tuple-element.17.refs_2_, ...), custom_call_target="tpu_custom_call" | custom-call | tf_op jit(solution)/shard_map/last/pallas_call | solution.py:761

commit v6 on v5

--- a/solution.py
+++ b/solution.py
@@ -70,10 +70,10 @@
 
     def all(self):
         return (
-            [self.sibling()]
-            + [self.at(dx=d) for d in (1, 2, 3)]
-            + [self.at(dy=d) for d in (1, 2, 3)]
-            + [self.at(dz=d) for d in range(1, 8)]
+            [self.at(dz=d) for d in (4, 3, 5, 2, 6, 1, 7)]
+            + [self.at(dy=d) for d in (2, 1, 3)]
+            + [self.at(dx=d) for d in (2, 1, 3)]
+            + [self.sibling()]
         )
 
 
@@ -719,13 +719,13 @@
         piece.drain()
 
 
-GATHER_STARTS = ((0, 0.0), (4, 3.4), (1, 8.0), (2, 11.5), (3, 15.0))
+GATHER_STARTS = ((0, 0.0), (4, 3.4), (1, 7.0), (2, 10.0), (3, 13.5))
 DIRECT = (0, 4)
 DIRECT_TIMES = (3.4, 0.8, 6.0, 0.9, 2.0, 0.0)
 GATHER_TIMES = (3.6, 0.8, 4.5, 4.0, 2.0, 0.0)
 EARLY = (2.5, 4.8, 5.0, 5.0, 5.5, 30.0, 0.0)
 LATE = (2.0, 4.5, 5.5, 5.5, 5.0, 30.0, 0.0)
-FINAL = (1.5, 4.3, 4.8, 4.2, 4.6, 30.0, 0.0)
+FINAL = (1.1, 4.3, 4.8, 4.2, 4.6, 30.0, 0.0)
 REDUCE_TIMES = (EARLY, EARLY, LATE, FINAL, (4.3,) + LATE[1:])
 SMALL_TIMES = (4.4, 4.6, 5.6, 25.0, 0.0)
 

time: 91.9 us -> 90.7 us (0.987)
  Pallas kernels: 90.2 us -> 88.8 us
    pallas_call x1, Pallas kernels: 87.8 us -> 86.5 us  [fused(): pl.pallas_call(kernel, out_shape=[jax.ShapeDtypeStruct((ROWS, D), BF16),...]
where the time goes in v6:
time: 90.7 us; the launch traced here: 90.3 us
  Pallas kernels  88.8 us (98%)
  between operations  1.47 us (2%)
    pallas_call x1, Pallas kernels, fused(): pl.pallas_call(kernel, out_shape=[jax.ShapeDtypeStruct((ROWS, D), BF16),...  86.5 us
    pallas_call x1, Pallas kernels, last(): pl.pallas_call(functools.partial(last_kernel, scale), out_shape=[jax.Shap...  2.35 us

profile of v6, /device:TPU:32, one launch (start us, length us, event | category | flops | bytes accessed | tf_op | source)
XLA Modules:
  0.0 90.3 jit_solution(16700687049813391876)
XLA Ops:
  1.3 86.5 %fused.1 = (bf16[384,1024]{1,0:T(8,128)(2,1)}, bf16[32,3072]{1,0:T(8,128)(2,1)}, bf16[32,1024]{1,0:T(8,128)(2,1)}, f32[1,32]{1,0:T(1,128)}, f32[1,32]{1,0:T(1,128)}) custom-call(s32[1]{0:T(128)S(6)} %copy.13.count_ref, s32[1,8]{1,0:T(1,128)} %starts_ref.1, bf16[384,1024]{1,0:T(8,128)(2,1)} %tok_ref.1, bf16[384,1024]{1,0:T(8,128)(2,1)} %cot_ref.1, ...), custom_call_target="tpu_custom_call" | custom-call | tf_op jit(solution)/shard_map/fused/pallas_call | solution.py:777
  87.7 2.3 %last.1 = (bf16[384,1024]{1,0:T(8,128)(2,1)}, f32[32,3072]{1,0:T(8,128)}, f32[32,1024]{1,0:T(8,128)}, f32[1,32]{1,0:T(1,128)}, f32[1,32]{1,0:T(1,128)}) custom-call(bf16[384,1024]{1,0:T(8,128)(2,1)} %get-tuple-element.15.refs_0_, bf16[32,3072]{1,0:T(8,128)(2,1)} %get-tuple-element.16.refs_1_, bf16[32,1024]{1,0:T(8,128)(2,1)} %get-tuple-element.17.refs_2_, ...), custom_call_target="tpu_custom_call" | custom-call | tf_op jit(solution)/shard_map/last/pallas_call | solution.py:761
